TPU v7x, 8 devices: a whole 2x2x1 slice. The times are simulated.
8 devices in a mesh: prob: 1 (over z), row: 2 (over y), col: 4 (over x, core).
Axes of the slice: x: 2, y: 2, z: 1, core: 2. Of those that a mesh axis runs over, the one named last changes fastest.
Arguments:
- kernel: bfloat16 [2048, 16384], P('row', 'col')
- cost_mat: bfloat16 [2048, 16384], P('row', 'col')
- src_mass: float32 [2048, 32], P('row', 'prob')
- tgt_mass: float32 [16384, 32], P('col', 'prob')
Outputs:
- output 1: float32 [2048, 32], P('row', 'prob')
- output 2: float32 [16384, 32], P('col', 'prob')
- output 3: float32 [32], P('prob')
All inputs are finite; a program needn't handle non-finite values.
Results may differ from a plain program's by a relative error of at most 0.001.
Values are sent between devices in bfloat16 or wider.
A program may use at most 1 GiB of HBM per device.

v0:
```python
import jax
import jax.numpy as jnp
from jax import lax
from jax.sharding import PartitionSpec as P

SWEEPS = 6


def solution(mesh):
    row_size = mesh.shape["row"]
    col_size = mesh.shape["col"]

    def local_fn(kernel, cost_mat, src_mass, tgt_mass):
        tgt_scale = jnp.ones(tgt_mass.shape, jnp.float32)
        for sweep_idx in range(SWEEPS):
            row_part = jnp.dot(kernel, tgt_scale.astype(jnp.bfloat16), preferred_element_type=jnp.float32)
            src_scale = src_mass / lax.psum(row_part, "col")
            col_part = lax.dot_general(kernel, src_scale.astype(jnp.bfloat16), (((0,), (0,)), ((), ())), preferred_element_type=jnp.float32)
            tgt_scale = tgt_mass / lax.psum(col_part, "row")
        weighted = jnp.dot(kernel * cost_mat, tgt_scale.astype(jnp.bfloat16), preferred_element_type=jnp.float32)
        part_cost = jnp.sum(src_scale * weighted, axis=0)
        mass_norm = float(kernel.shape[0] * row_size * kernel.shape[1] * col_size)
        return src_scale, tgt_scale, lax.psum(part_cost, ("row", "col")) / mass_norm

    return jax.shard_map(local_fn, mesh=mesh, in_specs=(P("row", "col"), P("row", "col"), P("row", "prob"), P("col", "prob")), out_specs=(P("row", "prob"), P("col", "prob"), P("prob")), check_vma=False)
```

profile of v0, /device:TPU:0, one launch (start us, length us, event | category | flops | bytes accessed | tf_op | source)
XLA Modules:
  0.0 421.8 jit_solution(16678639333984569294)
XLA Ops:
  7.2 0.0 copy-start.1
  7.2 0.0 all-reduce.13.cloned.1.call-start
  7.2 6.7 %convolution_bitcast_fusion.11 = f32[1024,32]{0,1:T(8,128)} fusion(bf16[1024,4096]{1,0:T(8,128)(2,1)} %param.4), kind=kOutput, calls=%fused_computation.13 | convolution fusion | flops 268435456 | bytes 8519680 | tf_op jit(solution)/shard_map/dot_general | solution.py:16
  13.9 0.0 copy-start
  13.9 0.0 all-reduce.13.cloned.1.call-update
  14.0 0.0 all-reduce.15.cloned.1.call-start
  14.0 29.1 %all-reduce.13.cloned.1.call-done = f32[1024,32]{0,1:T(8,128)} async-done(((f32[1024,32]{0,1:T(8,128)}), f32[1024,32]{0,1:T(8,128)}) %all-reduce.13.cloned.1.call-update) | async-done | bytes 131088 | tf_op jit(solution)/shard_map/psum | solution.py:17
  43.1 0.0 copy-done.1
  43.1 5.8 %convolution_bitcast_fusion.5 = f32[4096,32]{0,1:T(8,128)} fusion(bf16[1024,4096]{1,0:T(8,128)(2,1)} %param.4, f32[1024,32]{0,1:T(8,128)S(1)} %copy-done.1, f32[1024,32]{0,1:T(8,128)} %all-reduce.13.cloned.1.call-done), kind=kOutput, calls=%fused_computation.7 | convolution fusion | flops 268500992 | bytes 9175040 | tf_op jit(solution)/shard_map/dot_general | solution.py:18
  48.9 0.0 all-reduce.15.cloned.1.call-update
  48.9 0.0 all-reduce.17.cloned.1.call-start
  49.0 22.9 %all-reduce.15.cloned.1.call-done = f32[4096,32]{0,1:T(8,128)} async-done(((f32[4096,32]{0,1:T(8,128)}), f32[4096,32]{0,1:T(8,128)}) %all-reduce.15.cloned.1.call-update) | async-done | bytes 524304 | tf_op jit(solution)/shard_map/psum | solution.py:19
  71.9 0.0 copy-done
  71.9 6.8 %convolution_bitcast_fusion.10 = f32[1024,32]{0,1:T(8,128)} fusion(bf16[1024,4096]{1,0:T(8,128)(2,1)} %param.4, f32[4096,32]{0,1:T(8,128)S(1)} %copy-done, f32[4096,32]{0,1:T(8,128)} %all-reduce.15.cloned.1.call-done), kind=kOutput, calls=%fused_computation.12 | convolution fusion | flops 268697600 | bytes 9568256 | tf_op jit(solution)/shard_map/dot_general | solution.py:16
  78.7 0.0 all-reduce.17.cloned.1.call-update
  78.7 0.0 all-reduce.19.cloned.1.call-start
  78.8 26.2 %all-reduce.17.cloned.1.call-done = f32[1024,32]{0,1:T(8,128)} async-done(((f32[1024,32]{0,1:T(8,128)}), f32[1024,32]{0,1:T(8,128)}) %all-reduce.17.cloned.1.call-update) | async-done | bytes 131088 | tf_op jit(solution)/shard_map/psum | solution.py:17
  105.0 5.8 %convolution_bitcast_fusion.4 = f32[4096,32]{0,1:T(8,128)} fusion(bf16[1024,4096]{1,0:T(8,128)(2,1)} %param.4, f32[1024,32]{0,1:T(8,128)S(1)} %copy-done.1, f32[1024,32]{0,1:T(8,128)} %all-reduce.17.cloned.1.call-done), kind=kOutput, calls=%fused_computation.6 | convolution fusion | flops 268500992 | bytes 9175040 | tf_op jit(solution)/shard_map/dot_general | solution.py:18
  110.8 0.0 all-reduce.19.cloned.1.call-update
  110.8 0.0 all-reduce.21.cloned.1.call-start
  110.9 22.9 %all-reduce.19.cloned.1.call-done = f32[4096,32]{0,1:T(8,128)} async-done(((f32[4096,32]{0,1:T(8,128)}), f32[4096,32]{0,1:T(8,128)}) %all-reduce.19.cloned.1.call-update) | async-done | bytes 524304 | tf_op jit(solution)/shard_map/psum | solution.py:19
  133.8 6.8 %convolution_bitcast_fusion.9 = f32[1024,32]{0,1:T(8,128)} fusion(bf16[1024,4096]{1,0:T(8,128)(2,1)} %param.4, f32[4096,32]{0,1:T(8,128)S(1)} %copy-done, f32[4096,32]{0,1:T(8,128)} %all-reduce.19.cloned.1.call-done), kind=kOutput, calls=%fused_computation.11 | convolution fusion | flops 268697600 | bytes 9568256 | tf_op jit(solution)/shard_map/dot_general | solution.py:16
  140.7 0.0 all-reduce.21.cloned.1.call-update
  140.7 0.0 all-reduce.23.cloned.1.call-start
  140.7 26.2 %all-reduce.21.cloned.1.call-done = f32[1024,32]{0,1:T(8,128)} async-done(((f32[1024,32]{0,1:T(8,128)}), f32[1024,32]{0,1:T(8,128)}) %all-reduce.21.cloned.1.call-update) | async-done | bytes 131088 | tf_op jit(solution)/shard_map/psum | solution.py:17
  167.0 5.8 %convolution_bitcast_fusion.3 = f32[4096,32]{0,1:T(8,128)} fusion(bf16[1024,4096]{1,0:T(8,128)(2,1)} %param.4, f32[1024,32]{0,1:T(8,128)S(1)} %copy-done.1, f32[1024,32]{0,1:T(8,128)} %all-reduce.21.cloned.1.call-done), kind=kOutput, calls=%fused_computation.5 | convolution fusion | flops 268500992 | bytes 9175040 | tf_op jit(solution)/shard_map/dot_general | solution.py:18
  172.8 0.0 all-reduce.23.cloned.1.call-update
  172.8 0.0 all-reduce.25.cloned.1.call-start
  172.8 22.9 %all-reduce.23.cloned.1.call-done = f32[4096,32]{0,1:T(8,128)} async-done(((f32[4096,32]{0,1:T(8,128)}), f32[4096,32]{0,1:T(8,128)}) %all-reduce.23.cloned.1.call-update) | async-done | bytes 524304 | tf_op jit(solution)/shard_map/psum | solution.py:19
  195.8 6.8 %convolution_bitcast_fusion.8 = f32[1024,32]{0,1:T(8,128)} fusion(bf16[1024,4096]{1,0:T(8,128)(2,1)} %param.4, f32[4096,32]{0,1:T(8,128)S(1)} %copy-done, f32[4096,32]{0,1:T(8,128)} %all-reduce.23.cloned.1.call-done), kind=kOutput, calls=%fused_computation.10 | convolution fusion | flops 268697600 | bytes 9568256 | tf_op jit(solution)/shard_map/dot_general | solution.py:16
  202.6 0.0 all-reduce.25.cloned.1.call-update
  202.6 0.2 all-reduce.27.cloned.1.call-start
  202.8 26.1 %all-reduce.25.cloned.1.call-done = f32[1024,32]{0,1:T(8,128)} async-done(((f32[1024,32]{0,1:T(8,128)}), f32[1024,32]{0,1:T(8,128)}) %all-reduce.25.cloned.1.call-update) | async-done | bytes 131088 | tf_op jit(solution)/shard_map/psum | solution.py:17
  228.9 5.8 %convolution_bitcast_fusion.2 = f32[4096,32]{0,1:T(8,128)} fusion(bf16[1024,4096]{1,0:T(8,128)(2,1)} %param.4, f32[1024,32]{0,1:T(8,128)S(1)} %copy-done.1, f32[1024,32]{0,1:T(8,128)} %all-reduce.25.cloned.1.call-done), kind=kOutput, calls=%fused_computation.4 | convolution fusion | flops 268500992 | bytes 9175040 | tf_op jit(solution)/shard_map/dot_general | solution.py:18
  234.7 0.0 all-reduce.27.cloned.1.call-update
  234.7 0.0 all-reduce.29.cloned.1.call-start
  234.8 22.9 %all-reduce.27.cloned.1.call-done = f32[4096,32]{0,1:T(8,128)} async-done(((f32[4096,32]{0,1:T(8,128)}), f32[4096,32]{0,1:T(8,128)}) %all-reduce.27.cloned.1.call-update) | async-done | bytes 524304 | tf_op jit(solution)/shard_map/psum | solution.py:19
  257.7 6.8 %convolution_bitcast_fusion.7 = f32[1024,32]{0,1:T(8,128)} fusion(bf16[1024,4096]{1,0:T(8,128)(2,1)} %param.4, f32[4096,32]{0,1:T(8,128)S(1)} %copy-done, f32[4096,32]{0,1:T(8,128)} %all-reduce.27.cloned.1.call-done), kind=kOutput, calls=%fused_computation.9 | convolution fusion | flops 268697600 | bytes 9568256 | tf_op jit(solution)/shard_map/dot_general | solution.py:16
  264.5 0.0 all-reduce.29.cloned.1.call-update
  264.5 0.0 all-reduce.31.cloned.1.call-start
  264.6 26.2 %all-reduce.29.cloned.1.call-done = f32[1024,32]{0,1:T(8,128)} async-done(((f32[1024,32]{0,1:T(8,128)}), f32[1024,32]{0,1:T(8,128)}) %all-reduce.29.cloned.1.call-update) | async-done | bytes 131088 | tf_op jit(solution)/shard_map/psum | solution.py:17
  290.8 5.8 %convolution_bitcast_fusion.1 = f32[4096,32]{0,1:T(8,128)} fusion(bf16[1024,4096]{1,0:T(8,128)(2,1)} %param.4, f32[1024,32]{0,1:T(8,128)S(1)} %copy-done.1, f32[1024,32]{0,1:T(8,128)} %all-reduce.29.cloned.1.call-done), kind=kOutput, calls=%fused_computation.3 | convolution fusion | flops 268500992 | bytes 9175040 | tf_op jit(solution)/shard_map/dot_general | solution.py:18
  296.6 0.0 all-reduce.31.cloned.1.call-update
  296.6 0.0 all-reduce.33.cloned.1.call-start
  296.7 22.9 %all-reduce.31.cloned.1.call-done = f32[4096,32]{0,1:T(8,128)} async-done(((f32[4096,32]{0,1:T(8,128)}), f32[4096,32]{0,1:T(8,128)}) %all-reduce.31.cloned.1.call-update) | async-done | bytes 524304 | tf_op jit(solution)/shard_map/psum | solution.py:19
  319.6 6.8 %convolution_bitcast_fusion.6 = f32[1024,32]{0,1:T(8,128)} fusion(bf16[1024,4096]{1,0:T(8,128)(2,1)} %param.4, f32[4096,32]{0,1:T(8,128)S(1)} %copy-done, f32[4096,32]{0,1:T(8,128)} %all-reduce.31.cloned.1.call-done), kind=kOutput, calls=%fused_computation.8 | convolution fusion | flops 268697600 | bytes 9568256 | tf_op jit(solution)/shard_map/dot_general | solution.py:16
  326.5 0.0 all-reduce.33.cloned.1.call-update
  326.5 0.0 all-reduce.35.cloned.1.call-start
  326.5 26.2 %all-reduce.33.cloned.1.call-done = f32[1024,32]{0,1:T(8,128)} async-done(((f32[1024,32]{0,1:T(8,128)}), f32[1024,32]{0,1:T(8,128)}) %all-reduce.33.cloned.1.call-update) | async-done | bytes 131088 | tf_op jit(solution)/shard_map/psum | solution.py:17
  352.8 0.9 div.52
  353.7 0.0 copy-start.2
  353.7 5.8 %convolution_bitcast_fusion = f32[4096,32]{0,1:T(8,128)} fusion(bf16[1024,4096]{1,0:T(8,128)(2,1)} %param.4, f32[1024,32]{0,1:T(8,128)S(1)} %div.52), kind=kOutput, calls=%fused_computation.2 | convolution fusion | flops 268468224 | bytes 9043968 | tf_op jit(solution)/shard_map/dot_general | solution.py:18
  359.5 0.0 all-reduce.35.cloned.1.call-update
  359.5 23.0 %all-reduce.35.cloned.1.call-done = f32[4096,32]{0,1:T(8,128)} async-done(((f32[4096,32]{0,1:T(8,128)}), f32[4096,32]{0,1:T(8,128)}) %all-reduce.35.cloned.1.call-update) | async-done | bytes 524304 | tf_op jit(solution)/shard_map/psum | solution.py:19
  382.5 1.1 div.53
  383.6 0.0 copy-done.2
  383.6 0.0 copy-start.3
  383.6 8.5 %fusion.5 = f32[32]{0:T(128)S(1)} fusion(f32[1024,32]{0,1:T(8,128)S(1)} %div.52, bf16[1024,4096]{1,0:T(8,128)(2,1)} %param.4, bf16[1024,4096]{1,0:T(8,128)(2,1)} %param.5, f32[4096,32]{0,1:T(8,128)S(1)} %div.53), kind=kOutput, calls=%fused_computation.15 | convolution fusion | flops 272826336 | bytes 17432704 | tf_op jit(solution)/shard_map/dot_general | solution.py:20
  392.2 0.0 copy-done.3
  392.2 22.2 %psum.103 = f32[32]{0:T(128)S(1)} all-reduce(f32[32]{0:T(128)S(1)} %fusion.5), channel_id=1, replica_groups=mesh['prob'=1,'row'=2,'col'=4] {'row','col'}, use_global_device_ids=true, to_apply=%region_13.0 | all-reduce | flops 32 | bytes 256 | tf_op jit(solution)/shard_map/psum | solution.py:23
  414.4 0.5 broadcast_multiply_fusion
Async XLA Ops:
  7.2 35.9 %copy-start.1 = (f32[1024,32]{0,1:T(8,128)S(1)}, f32[1024,32]{0,1:T(8,128)}, u32[]{:S(2)}) copy-start(f32[1024,32]{0,1:T(8,128)} %param.6) | copy-start | bytes 393220
  7.2 35.9 %all-reduce.13.cloned.1.call-start = ((), (), s32[]{:S(2)}) async-start(), calls=%async_computation | async-start | bytes 262144 | tf_op jit(solution)/shard_map/psum | solution.py:17
  13.9 58.0 %copy-start = (f32[4096,32]{0,1:T(8,128)S(1)}, f32[4096,32]{0,1:T(8,128)}, u32[]{:S(2)}) copy-start(f32[4096,32]{0,1:T(8,128)} %param.7) | copy-start | bytes 1572868
  14.0 58.0 %all-reduce.15.cloned.1.call-start = ((), (), s32[]{:S(2)}) async-start(), calls=%async_computation.1 | async-start | bytes 1048576 | tf_op jit(solution)/shard_map/psum | solution.py:19
  48.9 56.1 %all-reduce.17.cloned.1.call-start = ((), (), s32[]{:S(2)}) async-start(), calls=%async_computation.2 | async-start | bytes 262144 | tf_op jit(solution)/shard_map/psum | solution.py:17
  78.7 55.1 %all-reduce.19.cloned.1.call-start = ((), (), s32[]{:S(2)}) async-start(), calls=%async_computation.3 | async-start | bytes 1048576 | tf_op jit(solution)/shard_map/psum | solution.py:19
  110.8 56.1 %all-reduce.21.cloned.1.call-start = ((), (), s32[]{:S(2)}) async-start(), calls=%async_computation.4 | async-start | bytes 262144 | tf_op jit(solution)/shard_map/psum | solution.py:17
  140.7 55.1 %all-reduce.23.cloned.1.call-start = ((), (), s32[]{:S(2)}) async-start(), calls=%async_computation.5 | async-start | bytes 1048576 | tf_op jit(solution)/shard_map/psum | solution.py:19
  172.8 56.1 %all-reduce.25.cloned.1.call-start = ((), (), s32[]{:S(2)}) async-start(), calls=%async_computation.6 | async-start | bytes 262144 | tf_op jit(solution)/shard_map/psum | solution.py:17
  202.6 55.1 %all-reduce.27.cloned.1.call-start = ((), (), s32[]{:S(2)}) async-start(), calls=%async_computation.7 | async-start | bytes 1048576 | tf_op jit(solution)/shard_map/psum | solution.py:19
  234.7 56.1 %all-reduce.29.cloned.1.call-start = ((), (), s32[]{:S(2)}) async-start(), calls=%async_computation.8 | async-start | bytes 262144 | tf_op jit(solution)/shard_map/psum | solution.py:17
  264.5 55.1 %all-reduce.31.cloned.1.call-start = ((), (), s32[]{:S(2)}) async-start(), calls=%async_computation.9 | async-start | bytes 1048576 | tf_op jit(solution)/shard_map/psum | solution.py:19
  296.6 56.1 %all-reduce.33.cloned.1.call-start = ((), (), s32[]{:S(2)}) async-start(), calls=%async_computation.10 | async-start | bytes 262144 | tf_op jit(solution)/shard_map/psum | solution.py:17
  326.5 56.0 %all-reduce.35.cloned.1.call-start = ((), (), s32[]{:S(2)}) async-start(), calls=%async_computation.11 | async-start | bytes 1048576 | tf_op jit(solution)/shard_map/psum | solution.py:19
  353.7 29.9 %copy-start.2 = (f32[1024,32]{0,1:T(8,128)}, f32[1024,32]{0,1:T(8,128)S(1)}, u32[]{:S(2)}) copy-start(f32[1024,32]{0,1:T(8,128)S(1)} %div.52) | copy-start | bytes 393220
  383.6 8.5 %copy-start.3 = (f32[4096,32]{0,1:T(8,128)}, f32[4096,32]{0,1:T(8,128)S(1)}, u32[]{:S(2)}) copy-start(f32[4096,32]{0,1:T(8,128)S(1)} %div.53) | copy-start | bytes 1572868
Sparse Core Ops, SparseCore 0:
  14.1 28.9 all-reduce.12
  49.0 22.8 all-reduce.14
  78.9 26.1 all-reduce.16
  111.0 22.8 all-reduce.18
  140.8 26.1 all-reduce.20
  172.9 22.8 all-reduce.22
  202.7 26.1 all-reduce.24
  234.8 22.8 all-reduce.26
  264.7 26.1 all-reduce.28
  296.8 22.8 all-reduce.30
  326.6 26.1 all-reduce.32
  359.6 22.8 all-reduce.34
where the time goes:
time: 422 us
  waiting for transfers between devices  298 us (71%)
  matrix products  84 us (20%)
  blocking collectives  22.2 us (5%)
  between operations  14.3 us (3%)
    psum x6, waiting for transfers between devices, local_fn(): src_scale = src_mass / lax.psum(row_part, 'col')  160 us
    psum x6, waiting for transfers between devices, local_fn(): tgt_scale = tgt_mass / lax.psum(col_part, 'row')  138 us
    dot_general x6, matrix products, local_fn(): jnp.dot(kernel, tgt_scale.astype(jnp.bfloat16), preferred_element_type=jn...  40.8 us
    dot_general x6, matrix products, local_fn(): lax.dot_general(kernel, src_scale.astype(jnp.bfloat16), (((0,), (0,)), ((...  34.7 us
    psum x1, blocking collectives, local_fn(): lax.psum(part_cost, ('row', 'col')) / mass_norm  22.2 us
    dot_general x1, matrix products, local_fn(): jnp.dot(kernel * cost_mat, tgt_scale.astype(jnp.bfloat16), preferred_elem...  8.52 us
  transfers between devices with their start and end apart: 12, of which 12 were waited for; matrix products, arithmetic and copies ran while one was open for 0% of the time, Pallas kernels for 0%

commit v1 on v0

v1 whole, which is shorter than its diff:
```python
import functools

import jax
import jax.numpy as jnp
from jax import lax
from jax.experimental import pallas as pl
from jax.experimental.pallas import tpu as pltpu
from jax.sharding import PartitionSpec as P

SWEEPS = 6
HALF_CHUNKS = 4
MESH = pl.DeviceIdType.MESH
F32 = jnp.float32
BF16 = jnp.bfloat16


def _dot_t(lhs, rhs):
    return lax.dot_general(lhs, rhs, (((1,), (1,)), ((), ())), preferred_element_type=F32)


def _kernel(norm, kern_hbm, cost_hbm, src_hbm, tgt_hbm, u_hbm, v_hbm, out_hbm,
            kern, cost, src, tgt, u_half, s_acc, s_out, s_in, x_out, x_in,
            t_out, t_own, t_in, v_out, v_in, t_full, v_full, w_acc, c_all, c_out,
            load_sem, tgt_sem, src_sem, store_sem, bar_dummy,
            sd_send, sd_recv, ud_send, ud_recv, sx_send, sx_recv,
            ty_send, ty_recv, vy_send, vy_recv, tf_send, tf_recv, c_send, c_recv):
    row = lax.axis_index("row")
    col = lax.axis_index("col")
    core = lax.rem(col, 2)
    chip = col // 2
    other_core = 1 - core
    other_row = 1 - row
    mate = {"col": chip * 2 + other_core}
    across = {"col": (1 - chip) * 2 + core}
    above = {"row": other_row}
    n_chunk, rows, width = kern.shape
    half = n_chunk // 2
    mid = rows // 2

    def load(hbm, buf, i):
        return pltpu.make_async_copy(hbm.at[:, pl.ds(i * width, width)], buf.at[i], load_sem.at[i])

    for i in range(n_chunk):
        load(kern_hbm, kern, i).start()
    src_copy = pltpu.make_async_copy(src_hbm.at[:, pl.ds(pl.multiple_of(core * mid, mid), mid)], src, src_sem)
    src_copy.start()
    for i in range(n_chunk):
        pltpu.make_async_copy(tgt_hbm.at[:, pl.ds(i * width, width)], tgt.at[i], tgt_sem.at[i]).start()

    barrier = pltpu.get_barrier_semaphore()
    me = row * 4 + col
    for d in range(1, 8):
        peer = lax.rem(me + d, 8)
        pl.semaphore_signal(barrier, inc=1, device_id={"row": peer // 4, "col": lax.rem(peer, 4)}, device_id_type=MESH)
    pl.semaphore_wait(barrier, 7)

    def remote(src_ref, dst_ref, send, recv, dev):
        return pltpu.make_async_remote_copy(src_ref=src_ref, dst_ref=dst_ref, send_sem=send, recv_sem=recv,
                                            device_id=dev, device_id_type=MESH)

    def reduce_rows(parity):
        s_out[0] = s_acc[:, 0:mid]
        s_out[1] = s_acc[:, mid:rows]
        to_mate = remote(s_out.at[other_core], s_in, sd_send, sd_recv, mate)
        to_mate.start()
        to_mate.wait_recv()
        chip_sum = s_out[core] + s_in[...]
        x_out[...] = chip_sum
        to_across = remote(x_out, x_in.at[parity], sx_send.at[parity], sx_recv.at[parity], across)
        to_across.start()
        to_across.wait_recv()
        u_half[core] = src[...] / (x_out[...] + x_in[parity])
        share = remote(u_half.at[core], u_half.at[core], ud_send, ud_recv, mate)
        share.start()
        to_mate.wait_send()
        to_across.wait_send()
        share.wait()

    def scaled_cols(u_lo, u_hi, i):
        return (jnp.dot(u_lo, kern[i, 0:mid, :], preferred_element_type=F32)
                + jnp.dot(u_hi, kern[i, mid:rows, :], preferred_element_type=F32))

    ones = jnp.ones((32, width), BF16)
    for i in range(n_chunk):
        load(kern_hbm, kern, i).wait()
        part = _dot_t(ones, kern[i])
        if i == 0:
            s_acc[...] = part
        else:
            s_acc[...] += part
    for i in range(n_chunk):
        load(cost_hbm, cost, i).start()
    src_copy.wait()
    for i in range(n_chunk):
        pltpu.make_async_copy(tgt_hbm.at[:, pl.ds(i * width, width)], tgt.at[i], tgt_sem.at[i]).wait()
    reduce_rows(0)

    def sweep(step, carry):
        u_lo = u_half[0].astype(BF16)
        u_hi = u_half[1].astype(BF16)
        sends = []
        for i in range(half):
            t_out[i] = scaled_cols(u_lo, u_hi, other_row * half + i)
            copy = remote(t_out.at[i], t_in.at[i], ty_send.at[i], ty_recv.at[i], above)
            copy.start()
            sends.append(copy)
        for i in range(half):
            t_own[i] = scaled_cols(u_lo, u_hi, row * half + i)
        shares = []
        for i in range(half):
            sends[i].wait_recv()
            v = tgt[row * half + i] / (t_own[i] + t_in[i])
            vb = v.astype(BF16)
            v_out[i] = vb
            copy = remote(v_out.at[i], v_in.at[i], vy_send.at[i], vy_recv.at[i], above)
            copy.start()
            shares.append(copy)
            part = _dot_t(vb, kern[row * half + i])
            if i == 0:
                s_acc[...] = part
            else:
                s_acc[...] += part
        for i in range(half):
            shares[i].wait_recv()
            s_acc[...] += _dot_t(v_in[i], kern[other_row * half + i])
        for i in range(half):
            sends[i].wait_send()
            shares[i].wait_send()
        reduce_rows(lax.rem(step + 1, 2))
        return carry

    lax.fori_loop(0, SWEEPS - 1, sweep, 0)

    u_lo = u_half[0].astype(BF16)
    u_hi = u_half[1].astype(BF16)
    lasts = []
    for i in range(n_chunk):
        t_full[i] = scaled_cols(u_lo, u_hi, i)
        copy = remote(t_full.at[i], v_full.at[i], tf_send.at[i], tf_recv.at[i], above)
        copy.start()
        lasts.append(copy)
    u_stores = [pltpu.make_async_copy(u_half.at[j], u_hbm.at[:, pl.ds(j * mid, mid)], store_sem.at[n_chunk + j]) for j in range(2)]
    for copy in u_stores:
        copy.start()
    for i in range(n_chunk):
        load(cost_hbm, cost, i).wait()
        cost[i] = kern[i] * cost[i]
    stores = []
    for i in range(n_chunk):
        lasts[i].wait_recv()
        v = tgt[i] / (t_full[i] + v_full[i])
        tgt[i] = v
        copy = pltpu.make_async_copy(tgt.at[i], v_hbm.at[:, pl.ds(i * width, width)], store_sem.at[i])
        copy.start()
        stores.append(copy)
        part = _dot_t(v.astype(BF16), cost[i])
        if i == 0:
            w_acc[...] = part
        else:
            w_acc[...] += part
    total = jnp.sum(u_half[0] * w_acc[:, 0:mid] + u_half[1] * w_acc[:, mid:rows], axis=1, keepdims=True)
    c_all[me] = jnp.broadcast_to(total, (32, 128))
    pieces = []
    for d in range(1, 8):
        peer = lax.rem(me + d, 8)
        copy = remote(c_all.at[me], c_all.at[me], c_send.at[d - 1], c_recv.at[d - 1],
                      {"row": peer // 4, "col": lax.rem(peer, 4)})
        copy.start()
        pieces.append(copy)
    for copy in lasts:
        copy.wait_send()
    for copy in pieces:
        copy.wait()
    grand = c_all[0]
    for j in range(1, 8):
        grand = grand + c_all[j]
    c_out[...] = grand / norm
    last = pltpu.make_async_copy(c_out, out_hbm, bar_dummy)
    last.start()
    for copy in u_stores + stores:
        copy.wait()
    last.wait()


def solution(mesh):
    row_size = mesh.shape["row"]
    col_size = mesh.shape["col"]

    def local_fn(kernel, cost_mat, src_mass, tgt_mass):
        rows, cols = kernel.shape
        q = src_mass.shape[1]
        n_chunk = 2 * HALF_CHUNKS
        width = cols // n_chunk
        mid = rows // 2
        norm = float(rows * row_size * cols * col_size)
        dma = pltpu.SemaphoreType.DMA
        anyspace = pl.BlockSpec(memory_space=pl.ANY)
        scratch = [
            pltpu.VMEM((n_chunk, rows, width), BF16),
            pltpu.VMEM((n_chunk, rows, width), BF16),
            pltpu.VMEM((q, mid), F32),
            pltpu.VMEM((n_chunk, q, width), F32),
            pltpu.VMEM((2, q, mid), F32),
            pltpu.VMEM((q, rows), F32),
            pltpu.VMEM((2, q, mid), F32),
            pltpu.VMEM((q, mid), F32),
            pltpu.VMEM((q, mid), F32),
            pltpu.VMEM((2, q, mid), F32),
            pltpu.VMEM((HALF_CHUNKS, q, width), F32),
            pltpu.VMEM((HALF_CHUNKS, q, width), F32),
            pltpu.VMEM((HALF_CHUNKS, q, width), F32),
            pltpu.VMEM((HALF_CHUNKS, q, width), BF16),
            pltpu.VMEM((HALF_CHUNKS, q, width), BF16),
            pltpu.VMEM((n_chunk, q, width), F32),
            pltpu.VMEM((n_chunk, q, width), F32),
            pltpu.VMEM((q, rows), F32),
            pltpu.VMEM((8, q, 128), F32),
            pltpu.VMEM((q, 128), F32),
            dma((n_chunk,)), dma((n_chunk,)), dma, dma((n_chunk + 2,)), dma,
            dma, dma, dma, dma, dma((2,)), dma((2,)),
            dma((HALF_CHUNKS,)), dma((HALF_CHUNKS,)), dma((HALF_CHUNKS,)), dma((HALF_CHUNKS,)),
            dma((n_chunk,)), dma((n_chunk,)), dma((7,)), dma((7,)),
        ]
        u_t, v_t, cost = pl.pallas_call(
            functools.partial(_kernel, norm),
            out_shape=(
                jax.ShapeDtypeStruct((q, rows), F32),
                jax.ShapeDtypeStruct((q, cols), F32),
                jax.ShapeDtypeStruct((q, 128), F32),
            ),
            in_specs=[anyspace] * 4,
            out_specs=(anyspace,) * 3,
            scratch_shapes=scratch,
            compiler_params=pltpu.CompilerParams(collective_id=0, has_side_effects=True, vmem_limit_bytes=48 * 1024 * 1024),
            name="sinkhorn",
        )(kernel, cost_mat, src_mass.T, tgt_mass.T)
        return u_t.T, v_t.T, cost[:, 0]

    return jax.shard_map(local_fn, mesh=mesh, in_specs=(P("row", "col"), P("row", "col"), P("row", "prob"), P("col", "prob")), out_specs=(P("row", "prob"), P("col", "prob"), P("prob")), check_vma=False)
```

time: 422 us -> 117 us (0.28)
  waiting for transfers between devices: 298 us -> 0 us
  Pallas kernels: 0 us -> 112 us
  matrix products: 84 us -> 0 us
  blocking collectives: 22.2 us -> 0 us
  between operations: 14.3 us -> 0.65 us
    psum x12 -> x0, waiting for transfers between devices: 298 us -> none  [the longest x6 160 us: local_fn(): src_scale = src_mass / lax.psum(row_part, 'col')]
    pallas_call x0 -> x1, Pallas kernels: none -> 112 us  [local_fn(): pl.pallas_call(functools.partial(_kernel, norm), out_shape=(jax.ShapeDtyp...]
    dot_general x13 -> x0, matrix products: 84 us -> none  [the longest x6 40.8 us: local_fn(): jnp.dot(kernel, tgt_scale.astype(jnp.bfloat16), preferred_element_type=jn...]
    psum x1 -> x0, blocking collectives: 22.2 us -> none  [local_fn(): lax.psum(part_cost, ('row', 'col')) / mass_norm]
  transfers between devices with their start and end apart: 12 -> 0, of which waited for: 12 -> 0; matrix products, arithmetic and copies ran while one was open for 0% -> 0% of each run, Pallas kernels for 0% -> 0%
where the time goes in v1:
time: 117 us
  Pallas kernels  112 us (96%)
  local copies, waits for them, and re-layouts  4.01 us (3%)
    pallas_call x1, Pallas kernels, local_fn(): pl.pallas_call(functools.partial(_kernel, norm), out_shape=(jax.ShapeDtyp...  112 us
    unnamed x6, local copies, waits for them, and re-layouts  3.39 us

profile of v1, /device:TPU:0, one launch (start us, length us, event | category | flops | bytes accessed | tf_op | source)
XLA Modules:
  0.0 117.1 jit_solution(6309885599067070927)
XLA Ops:
  0.6 0.0 copy-start
  0.6 1.0 copy-done
  1.7 0.0 copy-start.1
  1.7 0.9 copy-done.1
  2.6 112.4 %sinkhorn.1 = (f32[32,1024]{1,0:T(8,128)S(1)}, f32[32,4096]{1,0:T(8,128)S(1)}, f32[32,128]{1,0:T(8,128)S(1)}) custom-call(bf16[1024,4096]{1,0:T(8,128)(2,1)} %kern_hbm.1, bf16[1024,4096]{1,0:T(8,128)(2,1)} %cost_hbm.1, f32[32,1024]{1,0:T(8,128)S(1)} %bitcast.6, f32[32,4096]{1,0:T(8,128)S(1)} %bitcast.4), custom_call_target="tpu_custom_call" | custom-call | tf_op jit(solution)/shard_map/sinkhorn/pallas_call | solution.py:224
  115.0 0.6 slice_reduce_fusion
  115.6 0.7 copy.9
  116.3 0.8 copy.10
Async XLA Ops:
  0.6 1.0 copy-start
  1.7 0.9 copy-start.1

commit v2 on v0

v2 whole, which is shorter than its diff:
```python
import functools

import jax
import jax.numpy as jnp
from jax import lax
from jax.experimental import pallas as pl
from jax.experimental.pallas import tpu as pltpu
from jax.sharding import PartitionSpec as P

SWEEPS = 6
CHUNKS = 8
EARLY = 5
GROUPS = 2
MESH = pl.DeviceIdType.MESH
F32 = jnp.float32
BF16 = jnp.bfloat16


def _dot_t(lhs, rhs):
    return lax.dot_general(lhs, rhs, (((1,), (1,)), ((), ())), preferred_element_type=F32)


def _kernel(norm, kern_hbm, cost_hbm, src_hbm, tgt_hbm, u_hbm, v_hbm, out_hbm,
            kern, cost, src, tgt, u_all, s_acc, s_in, x_out, x_in, t_out, t_in, v_all, w_acc, c_all, c_out,
            load_sem, tgt_sem, src_sem, v_sem, u_sem, out_sem,
            s_send, s_recv, x_send, x_recv, t_send, t_recv, c_send, c_recv):
    row = lax.axis_index("row")
    col = lax.axis_index("col")
    core = lax.rem(col, 2)
    chip = col // 2
    mate = {"col": chip * 2 + (1 - core)}
    across = {"col": (1 - chip) * 2 + (1 - core)}
    above = {"row": 1 - row}
    n_chunk, rows, width = kern.shape
    q = t_out.shape[2]
    me = row * 4 + col

    def load(hbm, buf, i):
        return pltpu.make_async_copy(hbm.at[:, pl.ds(i * width, width)], buf.at[i], load_sem.at[i])

    def load_tgt(i):
        return pltpu.make_async_copy(tgt_hbm.at[:, pl.ds(i * width, width)], tgt.at[i], tgt_sem.at[i])

    for i in range(n_chunk):
        load(kern_hbm, kern, i).start()
    src_copy = pltpu.make_async_copy(src_hbm, src, src_sem)
    src_copy.start()
    for i in range(n_chunk):
        load_tgt(i).start()

    barrier = pltpu.get_barrier_semaphore()
    for d in range(1, 8):
        peer = lax.rem(me + d, 8)
        pl.semaphore_signal(barrier, inc=1, device_id={"row": peer // 4, "col": lax.rem(peer, 4)}, device_id_type=MESH)
    pl.semaphore_wait(barrier, 7)

    def remote(src_ref, dst_ref, send, recv, dev):
        return pltpu.make_async_remote_copy(src_ref=src_ref, dst_ref=dst_ref, send_sem=send, recv_sem=recv,
                                            device_id=dev, device_id_type=MESH)

    def pair_copy(g, p):
        return remote(s_acc.at[g], s_in.at[g, p], s_send.at[g], s_recv.at[g, p], mate)

    def chip_copy(g, p):
        return remote(x_out.at[g], x_in.at[g, p], x_send.at[g], x_recv.at[g, p], across)

    def row_copy(g, p, i):
        return remote(t_out.at[g, i], t_in.at[g, p, i], t_send.at[g, i], t_recv.at[g, p, i], above)

    def relay(g, p):
        pair_copy(g, p).wait_recv()
        x_out[g] = s_acc[g] + s_in[g, p]
        chip_copy(g, p).start()

    def finish(g, p, groups):
        chip_copy(g, p).wait_recv()
        total = x_out[g] + x_in[g, p]
        for h in groups:
            u_all[h] = src[h * q:(h + 1) * q] / total
        pair_copy(g, p).wait_send()
        chip_copy(g, p).wait_send()

    def send_cols(g, p):
        u = u_all[g].astype(BF16)
        for i in range(n_chunk):
            t_out[g, i] = jnp.dot(u, kern[i], preferred_element_type=F32)
            row_copy(g, p, i).start()

    def new_scale(g, p, i):
        row_copy(g, p, i).wait_recv()
        return tgt[i, g * q:(g + 1) * q] / (t_out[g, i] + t_in[g, p, i])

    def take_cols(g, p, lo, hi):
        for i in range(lo, hi):
            part = _dot_t(new_scale(g, p, i).astype(BF16), kern[i])
            if i == 0:
                s_acc[g] = part
            else:
                s_acc[g] += part
        if hi == n_chunk:
            pair_copy(g, 1 - p).start()
            for i in range(n_chunk):
                row_copy(g, p, i).wait_send()

    def take_last(g, p):
        for i in range(n_chunk):
            v = new_scale(g, p, i)
            v_all[i, g * q:(g + 1) * q] = v
            store_v(g, i).start()
            part = _dot_t(v.astype(BF16), cost[i])
            if i == 0:
                w_acc[g] = part
            else:
                w_acc[g] += part
        for i in range(n_chunk):
            row_copy(g, p, i).wait_send()
        c_all[me, g * q:(g + 1) * q] = jnp.broadcast_to(jnp.sum(u_all[g] * w_acc[g], axis=1, keepdims=True), (q, 128))

    def store_v(g, i):
        return pltpu.make_async_copy(v_all.at[i, pl.ds(g * q, q)], v_hbm.at[pl.ds(g * q, q), pl.ds(i * width, width)], v_sem.at[g, i])

    def store_u(g):
        return pltpu.make_async_copy(u_all.at[g], u_hbm.at[pl.ds(g * q, q)], u_sem.at[g])

    ones = jnp.ones((q, width), BF16)
    for i in range(n_chunk):
        load(kern_hbm, kern, i).wait()
        part = _dot_t(ones, kern[i])
        if i == 0:
            s_acc[0] = part
        else:
            s_acc[0] += part
    pair_copy(0, 0).start()
    for i in range(n_chunk):
        load(cost_hbm, cost, i).start()
    src_copy.wait()
    for i in range(n_chunk):
        load_tgt(i).wait()
    relay(0, 0)
    finish(0, 0, range(GROUPS))

    send_cols(0, 0)
    send_cols(1, 0)
    take_cols(0, 0, 0, n_chunk)
    relay(0, 1)
    take_cols(1, 0, 0, EARLY)
    finish(0, 1, (0,))

    def sweep(step, carry):
        p = lax.rem(step, 2)
        send_cols(0, p)
        take_cols(1, 1 - p, EARLY, n_chunk)
        relay(1, p)
        take_cols(0, p, 0, EARLY)
        finish(1, p, (1,))
        send_cols(1, p)
        take_cols(0, p, EARLY, n_chunk)
        relay(0, 1 - p)
        take_cols(1, p, 0, EARLY)
        finish(0, 1 - p, (0,))
        return carry

    lax.fori_loop(1, SWEEPS - 1, sweep, 0)

    p = (SWEEPS - 1) % 2
    send_cols(0, p)
    store_u(0).start()
    take_cols(1, 1 - p, EARLY, n_chunk)
    relay(1, p)
    for i in range(n_chunk):
        load(cost_hbm, cost, i).wait()
        cost[i] = kern[i] * cost[i]
    finish(1, p, (1,))
    send_cols(1, p)
    store_u(1).start()
    take_last(0, p)
    take_last(1, p)

    def share(d):
        peer = lax.rem(me + d, 8)
        return remote(c_all.at[me], c_all.at[me], c_send.at[d - 1], c_recv.at[d - 1],
                      {"row": peer // 4, "col": lax.rem(peer, 4)})

    for d in range(1, 8):
        share(d).start()
    for d in range(1, 8):
        share(d).wait()
    grand = c_all[0]
    for j in range(1, 8):
        grand = grand + c_all[j]
    c_out[...] = grand / norm
    last = pltpu.make_async_copy(c_out, out_hbm, out_sem)
    last.start()
    for g in range(GROUPS):
        store_u(g).wait()
        for i in range(n_chunk):
            store_v(g, i).wait()
    last.wait()


def solution(mesh):
    row_size = mesh.shape["row"]
    col_size = mesh.shape["col"]

    def local_fn(kernel, cost_mat, src_mass, tgt_mass):
        rows, cols = kernel.shape
        batch = src_mass.shape[1]
        q = batch // GROUPS
        width = cols // CHUNKS
        norm = float(rows * row_size * cols * col_size)
        dma = pltpu.SemaphoreType.DMA
        anyspace = pl.BlockSpec(memory_space=pl.ANY)
        scratch = [
            pltpu.VMEM((CHUNKS, rows, width), BF16),
            pltpu.VMEM((CHUNKS, rows, width), BF16),
            pltpu.VMEM((batch, rows), F32),
            pltpu.VMEM((CHUNKS, batch, width), F32),
            pltpu.VMEM((GROUPS, q, rows), F32),
            pltpu.VMEM((GROUPS, q, rows), F32),
            pltpu.VMEM((GROUPS, 2, q, rows), F32),
            pltpu.VMEM((GROUPS, q, rows), F32),
            pltpu.VMEM((GROUPS, 2, q, rows), F32),
            pltpu.VMEM((GROUPS, CHUNKS, q, width), F32),
            pltpu.VMEM((GROUPS, 2, CHUNKS, q, width), F32),
            pltpu.VMEM((CHUNKS, batch, width), F32),
            pltpu.VMEM((GROUPS, q, rows), F32),
            pltpu.VMEM((8, batch, 128), F32),
            pltpu.VMEM((batch, 128), F32),
            dma((CHUNKS,)), dma((CHUNKS,)), dma, dma((GROUPS, CHUNKS)), dma((GROUPS,)), dma,
            dma((GROUPS,)), dma((GROUPS, 2)), dma((GROUPS,)), dma((GROUPS, 2)),
            dma((GROUPS, CHUNKS)), dma((GROUPS, 2, CHUNKS)), dma((7,)), dma((7,)),
        ]
        u_t, v_t, cost = pl.pallas_call(
            functools.partial(_kernel, norm),
            out_shape=(
                jax.ShapeDtypeStruct((batch, rows), F32),
                jax.ShapeDtypeStruct((batch, cols), F32),
                jax.ShapeDtypeStruct((batch, 128), F32),
            ),
            in_specs=[anyspace] * 4,
            out_specs=(anyspace,) * 3,
            scratch_shapes=scratch,
            compiler_params=pltpu.CompilerParams(collective_id=0, has_side_effects=True, vmem_limit_bytes=48 * 1024 * 1024),
            name="sinkhorn",
        )(kernel, cost_mat, src_mass.T, tgt_mass.T)
        return u_t.T, v_t.T, cost[:, 0]

    return jax.shard_map(local_fn, mesh=mesh, in_specs=(P("row", "col"), P("row", "col"), P("row", "prob"), P("col", "prob")), out_specs=(P("row", "prob"), P("col", "prob"), P("prob")), check_vma=False)
```

time: 422 us -> 105 us (0.25)
  waiting for transfers between devices: 298 us -> 0 us
  Pallas kernels: 0 us -> 100 us
  matrix products: 84 us -> 0 us
  blocking collectives: 22.2 us -> 0 us
  between operations: 14.3 us -> 0.65 us
    psum x12 -> x0, waiting for transfers between devices: 298 us -> none  [the longest x6 160 us: local_fn(): src_scale = src_mass / lax.psum(row_part, 'col')]
    pallas_call x0 -> x1, Pallas kernels: none -> 100 us  [local_fn(): pl.pallas_call(functools.partial(_kernel, norm), out_shape=(jax.ShapeDtyp...]
    dot_general x13 -> x0, matrix products: 84 us -> none  [the longest x6 40.8 us: local_fn(): jnp.dot(kernel, tgt_scale.astype(jnp.bfloat16), preferred_element_type=jn...]
    psum x1 -> x0, blocking collectives: 22.2 us -> none  [local_fn(): lax.psum(part_cost, ('row', 'col')) / mass_norm]
  transfers between devices with their start and end apart: 12 -> 0, of which waited for: 12 -> 0; matrix products, arithmetic and copies ran while one was open for 0% -> 0% of each run, Pallas kernels for 0% -> 0%
where the time goes in v2:
time: 105 us
  Pallas kernels  100 us (95%)
  local copies, waits for them, and re-layouts  4.01 us (4%)
    pallas_call x1, Pallas kernels, local_fn(): pl.pallas_call(functools.partial(_kernel, norm), out_shape=(jax.ShapeDtyp...  100 us
    unnamed x6, local copies, waits for them, and re-layouts  3.39 us

profile of v2, /device:TPU:0, one launch (start us, length us, event | category | flops | bytes accessed | tf_op | source)
XLA Modules:
  0.0 104.8 jit_solution(1720127014402134544)
XLA Ops:
  0.6 0.0 copy-start
  0.6 1.0 copy-done
  1.7 0.0 copy-start.1
  1.7 0.9 copy-done.1
  2.6 100.1 %sinkhorn.1 = (f32[32,1024]{1,0:T(8,128)S(1)}, f32[32,4096]{1,0:T(8,128)S(1)}, f32[32,128]{1,0:T(8,128)S(1)}) custom-call(bf16[1024,4096]{1,0:T(8,128)(2,1)} %kern_hbm.1, bf16[1024,4096]{1,0:T(8,128)(2,1)} %cost_hbm.1, f32[32,1024]{1,0:T(8,128)S(1)} %bitcast.6, f32[32,4096]{1,0:T(8,128)S(1)} %bitcast.4), custom_call_target="tpu_custom_call" | custom-call | tf_op jit(solution)/shard_map/sinkhorn/pallas_call | solution.py:233
  102.7 0.6 slice_reduce_fusion
  103.3 0.7 copy.9
  104.0 0.8 copy.10
Async XLA Ops:
  0.6 1.0 copy-start
  1.7 0.9 copy-start.1

commit v3 on v2

--- a/solution.py
+++ b/solution.py
@@ -20,10 +20,19 @@
     return lax.dot_general(lhs, rhs, (((1,), (1,)), ((), ())), preferred_element_type=F32)
 
 
-def _kernel(norm, kern_hbm, cost_hbm, src_hbm, tgt_hbm, u_hbm, v_hbm, out_hbm,
-            kern, cost, src, tgt, u_all, s_acc, s_in, x_out, x_in, t_out, t_in, v_all, w_acc, c_all, c_out,
-            load_sem, tgt_sem, src_sem, v_sem, u_sem, out_sem,
-            s_send, s_recv, x_send, x_recv, t_send, t_recv, c_send, c_recv):
+def _emit(u_ref, v_ref, c_ref, u_hbm, v_hbm, c_out, sems):
+    copies = [pltpu.make_async_copy(u_ref, u_hbm, sems.at[0]), pltpu.make_async_copy(v_ref, v_hbm, sems.at[1])]
+    for copy in copies:
+        copy.start()
+    c_out[...] = c_ref[0, 0:c_out.shape[0]]
+    for copy in copies:
+        copy.wait()
+
+
+def _kernel(norm, kern_hbm, cost_hbm, src_hbm, tgt_hbm, u_out, v_out, c_out,
+            kern, kern_t, cost, src, tgt, u_all, s_acc, s_in, x_out, x_in, t_out, t_in, w_acc, c_all, z_all,
+            load_sem, tgt_sem, src_sem,
+            s_send, s_recv, x_send, x_recv, t_send, t_recv, c_send, c_recv, z_send, z_recv):
     row = lax.axis_index("row")
     col = lax.axis_index("col")
     core = lax.rem(col, 2)
@@ -72,11 +81,9 @@
         x_out[g] = s_acc[g] + s_in[g, p]
         chip_copy(g, p).start()
 
-    def finish(g, p, groups):
+    def finish(g, p):
         chip_copy(g, p).wait_recv()
-        total = x_out[g] + x_in[g, p]
-        for h in groups:
-            u_all[h] = src[h * q:(h + 1) * q] / total
+        u_all[g] = src[g * q:(g + 1) * q] / (x_out[g] + x_in[g, p])
         pair_copy(g, p).wait_send()
         chip_copy(g, p).wait_send()
 
@@ -92,7 +99,7 @@
 
     def take_cols(g, p, lo, hi):
         for i in range(lo, hi):
-            part = _dot_t(new_scale(g, p, i).astype(BF16), kern[i])
+            part = jnp.dot(new_scale(g, p, i).astype(BF16), kern_t[i], preferred_element_type=F32)
             if i == 0:
                 s_acc[g] = part
             else:
@@ -105,8 +112,7 @@
     def take_last(g, p):
         for i in range(n_chunk):
             v = new_scale(g, p, i)
-            v_all[i, g * q:(g + 1) * q] = v
-            store_v(g, i).start()
+            v_out[g * q:(g + 1) * q, i * width:(i + 1) * width] = v
             part = _dot_t(v.astype(BF16), cost[i])
             if i == 0:
                 w_acc[g] = part
@@ -114,37 +120,44 @@
                 w_acc[g] += part
         for i in range(n_chunk):
             row_copy(g, p, i).wait_send()
-        c_all[me, g * q:(g + 1) * q] = jnp.broadcast_to(jnp.sum(u_all[g] * w_acc[g], axis=1, keepdims=True), (q, 128))
-
-    def store_v(g, i):
-        return pltpu.make_async_copy(v_all.at[i, pl.ds(g * q, q)], v_hbm.at[pl.ds(g * q, q), pl.ds(i * width, width)], v_sem.at[g, i])
-
-    def store_u(g):
-        return pltpu.make_async_copy(u_all.at[g], u_hbm.at[pl.ds(g * q, q)], u_sem.at[g])
+        total = jnp.sum(u_all[g] * w_acc[g], axis=1, keepdims=True)
+        spot = lax.broadcasted_iota(jnp.int32, (q, 128), 0) + g * q == lax.broadcasted_iota(jnp.int32, (q, 128), 1)
+        return jnp.sum(jnp.where(spot, total, 0.0), axis=0, keepdims=True)
+
+    def share_first(d):
+        peer = lax.rem(col + d, 4)
+        return remote(z_all.at[col], z_all.at[col], z_send.at[d - 1], z_recv.at[d - 1], {"col": peer})
 
     ones = jnp.ones((q, width), BF16)
+    first = None
     for i in range(n_chunk):
         load(kern_hbm, kern, i).wait()
         part = _dot_t(ones, kern[i])
-        if i == 0:
-            s_acc[0] = part
-        else:
-            s_acc[0] += part
-    pair_copy(0, 0).start()
+        first = part if first is None else first + part
+    lanes = 128
+    z_all[col] = jnp.concatenate([first[0:1, k * lanes:(k + 1) * lanes] for k in range(rows // lanes)], axis=0)
+    for d in range(1, 4):
+        share_first(d).start()
     for i in range(n_chunk):
         load(cost_hbm, cost, i).start()
+    for i in range(n_chunk):
+        kern_t[i] = kern[i].T
     src_copy.wait()
     for i in range(n_chunk):
         load_tgt(i).wait()
-    relay(0, 0)
-    finish(0, 0, range(GROUPS))
+    for d in range(1, 4):
+        share_first(d).wait()
+    first_sum = (z_all[0] + z_all[1]) + (z_all[2] + z_all[3])
+    for g in range(GROUPS):
+        for k in range(rows // lanes):
+            u_all[g, :, k * lanes:(k + 1) * lanes] = src[g * q:(g + 1) * q, k * lanes:(k + 1) * lanes] / first_sum[k:k + 1, :]
 
     send_cols(0, 0)
     send_cols(1, 0)
     take_cols(0, 0, 0, n_chunk)
     relay(0, 1)
     take_cols(1, 0, 0, EARLY)
-    finish(0, 1, (0,))
+    finish(0, 1)
 
     def sweep(step, carry):
         p = lax.rem(step, 2)
@@ -152,29 +165,28 @@
         take_cols(1, 1 - p, EARLY, n_chunk)
         relay(1, p)
         take_cols(0, p, 0, EARLY)
-        finish(1, p, (1,))
+        finish(1, p)
         send_cols(1, p)
         take_cols(0, p, EARLY, n_chunk)
         relay(0, 1 - p)
         take_cols(1, p, 0, EARLY)
-        finish(0, 1 - p, (0,))
+        finish(0, 1 - p)
         return carry
 
     lax.fori_loop(1, SWEEPS - 1, sweep, 0)
 
     p = (SWEEPS - 1) % 2
     send_cols(0, p)
-    store_u(0).start()
+    u_out[0:q] = u_all[0]
     take_cols(1, 1 - p, EARLY, n_chunk)
     relay(1, p)
     for i in range(n_chunk):
         load(cost_hbm, cost, i).wait()
         cost[i] = kern[i] * cost[i]
-    finish(1, p, (1,))
+    finish(1, p)
     send_cols(1, p)
-    store_u(1).start()
-    take_last(0, p)
-    take_last(1, p)
+    u_out[q:2 * q] = u_all[1]
+    c_all[me] = jnp.broadcast_to(take_last(0, p) + take_last(1, p), (8, 128))
 
     def share(d):
         peer = lax.rem(me + d, 8)
@@ -189,13 +201,6 @@
     for j in range(1, 8):
         grand = grand + c_all[j]
     c_out[...] = grand / norm
-    last = pltpu.make_async_copy(c_out, out_hbm, out_sem)
-    last.start()
-    for g in range(GROUPS):
-        store_u(g).wait()
-        for i in range(n_chunk):
-            store_v(g, i).wait()
-    last.wait()
 
 
 def solution(mesh):
@@ -209,9 +214,11 @@
         width = cols // CHUNKS
         norm = float(rows * row_size * cols * col_size)
         dma = pltpu.SemaphoreType.DMA
-        anyspace = pl.BlockSpec(memory_space=pl.ANY)
+        hbm = pl.BlockSpec(memory_space=pltpu.HBM)
+        vmem = pl.BlockSpec(memory_space=pltpu.VMEM)
         scratch = [
             pltpu.VMEM((CHUNKS, rows, width), BF16),
+            pltpu.VMEM((CHUNKS, width, rows), BF16),
             pltpu.VMEM((CHUNKS, rows, width), BF16),
             pltpu.VMEM((batch, rows), F32),
             pltpu.VMEM((CHUNKS, batch, width), F32),
@@ -222,27 +229,33 @@
             pltpu.VMEM((GROUPS, 2, q, rows), F32),
             pltpu.VMEM((GROUPS, CHUNKS, q, width), F32),
             pltpu.VMEM((GROUPS, 2, CHUNKS, q, width), F32),
-            pltpu.VMEM((CHUNKS, batch, width), F32),
-            pltpu.VMEM((GROUPS, q, rows), F32),
-            pltpu.VMEM((8, batch, 128), F32),
-            pltpu.VMEM((batch, 128), F32),
-            dma((CHUNKS,)), dma((CHUNKS,)), dma, dma((GROUPS, CHUNKS)), dma((GROUPS,)), dma,
+            pltpu.VMEM((GROUPS, q, rows), F32),
+            pltpu.VMEM((8, 8, 128), F32),
+            pltpu.VMEM((4, 8, 128), F32),
+            dma((CHUNKS,)), dma((CHUNKS,)), dma,
             dma((GROUPS,)), dma((GROUPS, 2)), dma((GROUPS,)), dma((GROUPS, 2)),
-            dma((GROUPS, CHUNKS)), dma((GROUPS, 2, CHUNKS)), dma((7,)), dma((7,)),
+            dma((GROUPS, CHUNKS)), dma((GROUPS, 2, CHUNKS)), dma((7,)), dma((7,)), dma((3,)), dma((3,)),
         ]
+        u_shape = jax.ShapeDtypeStruct((batch, rows), F32)
+        v_shape = jax.ShapeDtypeStruct((batch, cols), F32)
         u_t, v_t, cost = pl.pallas_call(
             functools.partial(_kernel, norm),
-            out_shape=(
-                jax.ShapeDtypeStruct((batch, rows), F32),
-                jax.ShapeDtypeStruct((batch, cols), F32),
-                jax.ShapeDtypeStruct((batch, 128), F32),
-            ),
-            in_specs=[anyspace] * 4,
-            out_specs=(anyspace,) * 3,
+            out_shape=(u_shape, v_shape, jax.ShapeDtypeStruct((8, 128), F32)),
+            in_specs=[hbm] * 4,
+            out_specs=(vmem,) * 3,
             scratch_shapes=scratch,
             compiler_params=pltpu.CompilerParams(collective_id=0, has_side_effects=True, vmem_limit_bytes=48 * 1024 * 1024),
             name="sinkhorn",
-        )(kernel, cost_mat, src_mass.T, tgt_mass.T)
-        return u_t.T, v_t.T, cost[:, 0]
+        )(kernel, cost_mat, pltpu.with_memory_space_constraint(src_mass.T, pltpu.HBM), pltpu.with_memory_space_constraint(tgt_mass.T, pltpu.HBM))
+        u_t, v_t, cost = pl.pallas_call(
+            _emit,
+            out_shape=(u_shape, v_shape, jax.ShapeDtypeStruct((batch,), F32)),
+            in_specs=[vmem] * 3,
+            out_specs=(hbm, hbm, vmem),
+            scratch_shapes=[dma((2,))],
+            compiler_params=pltpu.CompilerParams(vmem_limit_bytes=4 * 1024 * 1024),
+            name="emit",
+        )(u_t, v_t, cost)
+        return u_t.T, v_t.T, cost
 
     return jax.shard_map(local_fn, mesh=mesh, in_specs=(P("row", "col"), P("row", "col"), P("row", "prob"), P("col", "prob")), out_specs=(P("row", "prob"), P("col", "prob"), P("prob")), check_vma=False)

time: 105 us -> 96.6 us (0.920)
  Pallas kernels: 100 us -> 95.7 us
  local copies, waits for them, and re-layouts: 4.01 us -> 0 us
    pallas_call x1 -> x2, Pallas kernels: 100 us -> 95.7 us  [the longest x1 94.3 us: local_fn(): pl.pallas_call(functools.partial(_kernel, norm), out_shape=(u_shape, v_sh...]
    unnamed x6 -> x0, local copies, waits for them, and re-layouts: 3.39 us -> none
where the time goes in v3:
time: 96.6 us; the launch traced here: 96.5 us
  Pallas kernels  95.7 us (99%)
    pallas_call x1, Pallas kernels, local_fn(): pl.pallas_call(functools.partial(_kernel, norm), out_shape=(u_shape, v_sh...  94.3 us

profile of v3, /device:TPU:0, one launch (start us, length us, event | category | flops | bytes accessed | tf_op | source)
XLA Modules:
  0.0 96.5 jit_solution(17696544298397830256)
XLA Ops:
  0.6 94.3 %sinkhorn.1 = (f32[32,1024]{1,0:T(8,128)S(1)}, f32[32,4096]{1,0:T(8,128)S(1)}, f32[8,128]{1,0:T(8,128)S(1)}) custom-call(bf16[1024,4096]{1,0:T(8,128)(2,1)} %kern_hbm.1, bf16[1024,4096]{1,0:T(8,128)(2,1)} %cost_hbm.1, f32[32,1024]{1,0:T(8,128)} %bitcast.5, f32[32,4096]{1,0:T(8,128)} %bitcast.4), custom_call_target="tpu_custom_call" | custom-call | tf_op jit(solution)/shard_map/sinkhorn/pallas_call | solution.py:241
  94.9 1.4 %emit.1 = (f32[32,1024]{1,0:T(8,128)}, f32[32,4096]{1,0:T(8,128)}, f32[32]{0:T(128)}) custom-call(f32[32,1024]{1,0:T(8,128)S(1)} %get-tuple-element.9.u_ref, f32[32,4096]{1,0:T(8,128)S(1)} %get-tuple-element.10.v_ref, f32[8,128]{1,0:T(8,128)S(1)} %get-tuple-element.11.c_ref), custom_call_target="tpu_custom_call" | custom-call | tf_op jit(solution)/shard_map/emit/pallas_call | solution.py:250

commit v4 on v3

v4 whole, which is shorter than its diff:
```python
import functools

import jax
import jax.numpy as jnp
from jax import lax
from jax.experimental import pallas as pl
from jax.experimental.pallas import tpu as pltpu
from jax.sharding import PartitionSpec as P

SWEEPS = 6
LOADS = 8
GROUPS = 2
STEP = 512
DIRECT = 4
TURN = 2
EARLY = 3
MIDDLE = 1
MIX = (1, 1, 1)
FIRST_MIX = ()
LAST_EARLY = 4
LAST_MIX = (2, 2, 2)
MESH = pl.DeviceIdType.MESH
F32 = jnp.float32
BF16 = jnp.bfloat16


def _dot(lhs, rhs):
    return jnp.dot(lhs, rhs, preferred_element_type=F32)


def _dot_t(lhs, rhs):
    return lax.dot_general(lhs, rhs, (((1,), (1,)), ((), ())), preferred_element_type=F32)


def _emit(u_ref, v_ref, c_ref, u_hbm, v_hbm, c_hbm, c_row, sems):
    c_row[...] = c_ref[0, 0:c_row.shape[0]]
    copies = [pltpu.make_async_copy(v_ref, v_hbm, sems.at[1]), pltpu.make_async_copy(u_ref, u_hbm, sems.at[0]),
              pltpu.make_async_copy(c_row, c_hbm, sems.at[2])]
    for copy in copies:
        copy.start()
    for copy in copies:
        copy.wait()


def _kernel(norm, kern_hbm, cost_hbm, src_hbm, tgt_hbm, u_out, v_out, c_out,
            kern, kern_t, cost, src, tgt, u_all, s_acc, lo_in, hi_in, x_out, x_in, t_out, t_in, vb_out, vb_in, w_acc, c_all, z_all,
            load_sem, tgt_sem, src_sem, lo_send, lo_recv, hi_send, hi_recv, x_send, x_recv,
            t_send, t_recv, v_send, v_recv, f_send, f_recv, c_send, c_recv, z_send, z_recv):
    row = lax.axis_index("row")
    col = lax.axis_index("col")
    core = lax.rem(col, 2)
    chip = col // 2
    mate = {"col": chip * 2 + (1 - core)}
    across = {"col": (1 - chip) * 2 + (1 - core)}
    level = {"col": (1 - chip) * 2 + core}
    above = {"row": 1 - row}
    rows, cols = kern.shape
    mid = rows // 2
    q = t_out.shape[1]
    me = row * 4 + col
    wide = cols // LOADS
    base = DIRECT * STEP
    n_last = cols // STEP

    def load(hbm, buf, i):
        part = pl.ds(i * wide, wide)
        return pltpu.make_async_copy(hbm.at[:, part], buf.at[:, part], load_sem.at[i])

    for i in range(LOADS):
        load(kern_hbm, kern, i).start()
    src_copy = pltpu.make_async_copy(src_hbm, src, src_sem)
    src_copy.start()
    tgt_copy = pltpu.make_async_copy(tgt_hbm, tgt, tgt_sem)
    tgt_copy.start()

    barrier = pltpu.get_barrier_semaphore()
    for d in range(1, 8):
        peer = lax.rem(me + d, 8)
        pl.semaphore_signal(barrier, inc=1, device_id={"row": peer // 4, "col": lax.rem(peer, 4)}, device_id_type=MESH)
    pl.semaphore_wait(barrier, 7)

    def remote(src_ref, dst_ref, send, recv, dev):
        return pltpu.make_async_remote_copy(src_ref=src_ref, dst_ref=dst_ref, send_sem=send, recv_sem=recv,
                                            device_id=dev, device_id_type=MESH)

    def turn_cols(owner, k):
        return pl.ds(pl.multiple_of(base + owner * (TURN * STEP) + k * STEP, STEP), STEP)

    def turn_slot(owner, k):
        return pl.ds(pl.multiple_of(owner * (TURN * STEP) + k * STEP, STEP), STEP)

    def line(i):
        return pl.ds(i * STEP, STEP)


    def lo_copies(g, p):
        return [remote(s_acc.at[g, :, pl.ds(0, mid)], lo_in.at[g, p, col], lo_send.at[g, j], lo_recv.at[g, p, j], dev)
                for j, dev in enumerate((across, level, mate))]

    def hi_copy(g, p):
        return remote(s_acc.at[g, :, pl.ds(mid, mid)], hi_in.at[g, p], hi_send.at[g], hi_recv.at[g, p], mate)

    def chip_copy(g, p):
        return remote(x_out.at[g], x_in.at[g, p], x_send.at[g], x_recv.at[g, p], across)

    def spread(g, p):
        hi_copy(g, p).start()
        for copy in lo_copies(g, p):
            copy.start()
        lo_in[g, p, col] = s_acc[g, :, 0:mid]

    def relay(g, p):
        hi_copy(g, p).wait_recv()
        x_out[g] = s_acc[g, :, mid:rows] + hi_in[g, p]
        chip_copy(g, p).start()

    def finish_lo(g, p):
        for copy in lo_copies(g, p):
            copy.wait_recv()
        total = (lo_in[g, p, 0] + lo_in[g, p, 1]) + (lo_in[g, p, 2] + lo_in[g, p, 3])
        u_all[g, :, 0:mid] = src[g * q:(g + 1) * q, 0:mid] / total

    def start_cols(g):
        u = u_all[g, :, 0:mid].astype(BF16)
        for i in range(n_last):
            t_out[g, :, line(i)] = _dot(u, kern[0:mid, line(i)])

    def finish_hi(g, p):
        chip_copy(g, p).wait_recv()
        u_all[g, :, mid:rows] = src[g * q:(g + 1) * q, mid:rows] / (x_out[g] + x_in[g, p])

    def settle(g, p):
        hi_copy(g, p).wait_send()
        chip_copy(g, p).wait_send()
        for copy in lo_copies(g, p):
            copy.wait_send()


    def add_cols(g, part):
        t_out[g, :, part] += _dot(u_all[g, :, mid:rows].astype(BF16), kern[mid:rows, part])

    def t_copy(g, p, i):
        part = turn_cols(1 - row, i) if i < TURN else line(i - TURN)
        return remote(t_out.at[g, :, part], t_in.at[g, p, :, part], t_send.at[g, i], t_recv.at[g, p, i], above)

    def v_copy(g, k):
        part = turn_slot(row, k)
        return remote(vb_out.at[g, :, part], vb_in.at[g, :, part], v_send.at[g, k], v_recv.at[g, k], above)

    def f_copy(g, p, i):
        return remote(t_out.at[g, :, line(i)], t_in.at[g, p, :, line(i)], f_send.at[g, i], f_recv.at[g, i], above)

    def send_ops(g, p):
        def send(i):
            add_cols(g, turn_cols(1 - row, i) if i < TURN else line(i - TURN))
            t_copy(g, p, i).start()

        def keep(k):
            add_cols(g, turn_cols(row, k))

        return [functools.partial(send, i) for i in range(TURN + DIRECT)] + [functools.partial(keep, k) for k in range(TURN)]

    def last_send_ops(g, p):
        def send(i):
            add_cols(g, line(i))
            f_copy(g, p, i).start()

        return [functools.partial(send, i) for i in range(n_last)]

    def gather(g, vb, part, first):
        got = _dot(vb, kern_t[part])
        if first:
            s_acc[g] = got
        else:
            s_acc[g] += got

    def take_ops(g, p):
        def own(k):
            t_copy(g, p, k).wait_recv()
            part = turn_cols(row, k)
            vb = (tgt[g * q:(g + 1) * q, part] / (t_out[g, :, part] + t_in[g, p, :, part])).astype(BF16)
            vb_out[g, :, turn_slot(row, k)] = vb
            v_copy(g, k).start()
            gather(g, vb, part, k == 0)

        def both(i):
            t_copy(g, p, TURN + i).wait_recv()
            part = line(i)
            vb = (tgt[g * q:(g + 1) * q, part] / (t_out[g, :, part] + t_in[g, p, :, part])).astype(BF16)
            gather(g, vb, part, False)

        def back(k):
            v_copy(g, k).wait_recv()
            gather(g, vb_in[g, :, turn_slot(1 - row, k)], turn_cols(1 - row, k), False)
            if k == TURN - 1:
                spread(g, 1 - p)

        return ([functools.partial(own, k) for k in range(TURN)] + [functools.partial(both, i) for i in range(DIRECT)]
                + [functools.partial(back, k) for k in range(TURN)])

    def last_take_ops(g, p):
        def take(i):
            f_copy(g, p, i).wait_recv()
            part = line(i)
            v = tgt[g * q:(g + 1) * q, part] / (t_out[g, :, part] + t_in[g, p, :, part])
            v_out[g * q:(g + 1) * q, part] = v
            got = _dot_t(v.astype(BF16), cost[:, part])
            if i == 0:
                w_acc[g] = got
            else:
                w_acc[g] += got

        return [functools.partial(take, i) for i in range(n_last)]

    def sent(g, p):
        for i in range(TURN + DIRECT):
            t_copy(g, p, i).wait_send()
        for k in range(TURN):
            v_copy(g, k).wait_send()

    def run(ops):
        for op in ops:
            op()

    def merge(sends, takes, mix):
        sends, takes = list(sends), list(takes)
        for count in mix:
            run(sends[:count])
            sends = sends[count:]
            run(takes[:1])
            takes = takes[1:]
        while sends or takes:
            run(sends[:1] + takes[:1])
            sends, takes = sends[1:], takes[1:]

    def cost_row(g):
        total = jnp.sum(u_all[g] * w_acc[g], axis=1, keepdims=True)
        spot = lax.broadcasted_iota(jnp.int32, (q, 128), 0) + g * q == lax.broadcasted_iota(jnp.int32, (q, 128), 1)
        return jnp.sum(jnp.where(spot, total, 0.0), axis=0, keepdims=True)


    def share_first(d):
        peer = lax.rem(col + d, 4)
        return remote(z_all.at[col], z_all.at[col], z_send.at[d - 1], z_recv.at[d - 1], {"col": peer})

    ones = jnp.ones((q, wide), BF16)
    first = None
    for i in range(LOADS):
        load(kern_hbm, kern, i).wait()
        part = _dot_t(ones, kern[:, i * wide:(i + 1) * wide])
        first = part if first is None else first + part
    lanes = 128
    z_all[col] = jnp.concatenate([first[0:1, k * lanes:(k + 1) * lanes] for k in range(rows // lanes)], axis=0)
    for d in range(1, 4):
        share_first(d).start()
    for i in range(LOADS):
        load(cost_hbm, cost, i).start()
    for i in range(LOADS):
        kern_t[i * wide:(i + 1) * wide] = kern[:, i * wide:(i + 1) * wide].T
    src_copy.wait()
    tgt_copy.wait()
    for d in range(1, 4):
        share_first(d).wait()
    first_sum = (z_all[0] + z_all[1]) + (z_all[2] + z_all[3])
    for g in range(GROUPS):
        for k in range(rows // lanes):
            u_all[g, :, k * lanes:(k + 1) * lanes] = src[g * q:(g + 1) * q, k * lanes:(k + 1) * lanes] / first_sum[k:k + 1, :]

    seen = EARLY + MIDDLE
    start_cols(0)
    run(send_ops(0, 0))
    start_cols(1)
    run(take_ops(0, 0)[:TURN])
    merge(send_ops(1, 0), take_ops(0, 0)[TURN:], FIRST_MIX)
    relay(0, 1)
    sent(0, 0)
    run(take_ops(1, 0)[:EARLY])
    finish_lo(0, 1)
    start_cols(0)
    run(take_ops(1, 0)[EARLY:seen])
    finish_hi(0, 1)

    def sweep(step, carry):
        p = lax.rem(step, 2)
        for g, pg, ph in ((0, p, 1 - p), (1, p, p)):
            h = 1 - g
            merge(send_ops(g, pg), take_ops(h, ph)[seen:], MIX)
            settle(g, pg)
            sent(h, ph)
            relay(h, 1 - ph)
            run(take_ops(g, pg)[:EARLY])
            finish_lo(h, 1 - ph)
            start_cols(h)
            run(take_ops(g, pg)[EARLY:seen])
            finish_hi(h, 1 - ph)
        return carry

    lax.fori_loop(1, SWEEPS - 1, sweep, 0)

    p = (SWEEPS - 1) % 2
    merge(last_send_ops(0, p), take_ops(1, 1 - p)[seen:], MIX)
    settle(0, p)
    u_out[0:q] = u_all[0]
    sent(1, 1 - p)
    relay(1, p)
    for i in range(LOADS):
        load(cost_hbm, cost, i).wait()
    cost[...] = kern[...] * cost[...]
    takes = last_take_ops(0, p)
    run(takes[:LAST_EARLY])
    finish_lo(1, p)
    start_cols(1)
    finish_hi(1, p)
    merge(last_send_ops(1, p), takes[LAST_EARLY:], LAST_MIX)
    settle(1, p)
    u_out[q:2 * q] = u_all[1]
    run(last_take_ops(1, p))
    for g in range(GROUPS):
        for i in range(n_last):
            f_copy(g, p, i).wait_send()
    c_all[me] = jnp.broadcast_to(cost_row(0) + cost_row(1), (8, 128))

    def share(d):
        peer = lax.rem(me + d, 8)
        return remote(c_all.at[me], c_all.at[me], c_send.at[d - 1], c_recv.at[d - 1],
                      {"row": peer // 4, "col": lax.rem(peer, 4)})

    for d in range(1, 8):
        share(d).start()
    for d in range(1, 8):
        share(d).wait()
    grand = c_all[0]
    for j in range(1, 8):
        grand = grand + c_all[j]
    c_out[...] = grand / norm


def solution(mesh):
    row_size = mesh.shape["row"]
    col_size = mesh.shape["col"]

    def local_fn(kernel, cost_mat, src_mass, tgt_mass):
        rows, cols = kernel.shape
        batch = src_mass.shape[1]
        q = batch // GROUPS
        mid = rows // 2
        norm = float(rows * row_size * cols * col_size)
        dma = pltpu.SemaphoreType.DMA
        hbm = pl.BlockSpec(memory_space=pltpu.HBM)
        vmem = pl.BlockSpec(memory_space=pltpu.VMEM)
        turn = 2 * TURN * STEP
        scratch = [
            pltpu.VMEM((rows, cols), BF16),
            pltpu.VMEM((cols, rows), BF16),
            pltpu.VMEM((rows, cols), BF16),
            pltpu.VMEM((batch, rows), F32),
            pltpu.VMEM((batch, cols), F32),
            pltpu.VMEM((GROUPS, q, rows), F32),
            pltpu.VMEM((GROUPS, q, rows), F32),
            pltpu.VMEM((GROUPS, 2, 4, q, mid), F32),
            pltpu.VMEM((GROUPS, 2, q, mid), F32),
            pltpu.VMEM((GROUPS, q, mid), F32),
            pltpu.VMEM((GROUPS, 2, q, mid), F32),
            pltpu.VMEM((GROUPS, q, cols), F32),
            pltpu.VMEM((GROUPS, 2, q, cols), F32),
            pltpu.VMEM((GROUPS, q, turn), BF16),
            pltpu.VMEM((GROUPS, q, turn), BF16),
            pltpu.VMEM((GROUPS, q, rows), F32),
            pltpu.VMEM((8, 8, 128), F32),
            pltpu.VMEM((4, 8, 128), F32),
            dma((LOADS,)), dma, dma,
            dma((GROUPS, 3)), dma((GROUPS, 2, 3)), dma((GROUPS,)), dma((GROUPS, 2)), dma((GROUPS,)), dma((GROUPS, 2)),
            dma((GROUPS, TURN + DIRECT)), dma((GROUPS, 2, TURN + DIRECT)), dma((GROUPS, TURN)), dma((GROUPS, TURN)),
            dma((GROUPS, cols // STEP)), dma((GROUPS, cols // STEP)), dma((7,)), dma((7,)), dma((3,)), dma((3,)),
        ]
        u_shape = jax.ShapeDtypeStruct((batch, rows), F32)
        v_shape = jax.ShapeDtypeStruct((batch, cols), F32)
        u_t, v_t, cost = pl.pallas_call(
            functools.partial(_kernel, norm),
            out_shape=(u_shape, v_shape, jax.ShapeDtypeStruct((8, 128), F32)),
            in_specs=[hbm] * 4,
            out_specs=(vmem,) * 3,
            scratch_shapes=scratch,
            compiler_params=pltpu.CompilerParams(collective_id=0, has_side_effects=True, vmem_limit_bytes=48 * 1024 * 1024),
            name="sinkhorn",
        )(kernel, cost_mat, pltpu.with_memory_space_constraint(src_mass.T, pltpu.HBM), pltpu.with_memory_space_constraint(tgt_mass.T, pltpu.HBM))
        u_t, v_t, cost = pl.pallas_call(
            _emit,
            out_shape=(u_shape, v_shape, jax.ShapeDtypeStruct((batch,), F32)),
            in_specs=[vmem] * 3,
            out_specs=(hbm,) * 3,
            scratch_shapes=[pltpu.VMEM((batch,), F32), dma((3,))],
            compiler_params=pltpu.CompilerParams(vmem_limit_bytes=4 * 1024 * 1024),
            name="emit",
        )(u_t, v_t, cost)
        return u_t.T, v_t.T, cost

    return jax.shard_map(local_fn, mesh=mesh, in_specs=(P("row", "col"), P("row", "col"), P("row", "prob"), P("col", "prob")), out_specs=(P("row", "prob"), P("col", "prob"), P("prob")), check_vma=False)
```

time: 96.6 us -> 88.6 us (0.917)
  Pallas kernels: 95.7 us -> 87.7 us
    pallas_call x1, Pallas kernels: 94.3 us -> 86.9 us  [local_fn(): pl.pallas_call(functools.partial(_kernel, norm), out_shape=(u_shape, v_sh...]
where the time goes in v4:
time: 88.6 us; the launch traced here: 88.5 us
  Pallas kernels  87.7 us (99%)
    pallas_call x1, Pallas kernels, local_fn(): pl.pallas_call(functools.partial(_kernel, norm), out_shape=(u_shape, v_sh...  86.9 us

profile of v4, /device:TPU:0, one launch (start us, length us, event | category | flops | bytes accessed | tf_op | source)
XLA Modules:
  0.0 88.5 jit_solution(18070495071136998595)
XLA Ops:
  0.6 86.9 %sinkhorn.1 = (f32[32,1024]{1,0:T(8,128)S(1)}, f32[32,4096]{1,0:T(8,128)S(1)}, f32[8,128]{1,0:T(8,128)S(1)}) custom-call(bf16[1024,4096]{1,0:T(8,128)(2,1)} %kern_hbm.1, bf16[1024,4096]{1,0:T(8,128)(2,1)} %cost_hbm.1, f32[32,1024]{1,0:T(8,128)} %bitcast.5, f32[32,4096]{1,0:T(8,128)} %bitcast.4), custom_call_target="tpu_custom_call" | custom-call | tf_op jit(solution)/shard_map/sinkhorn/pallas_call | solution.py:378
  87.5 0.9 emit.1

commit v5 on v4

--- a/solution.py
+++ b/solution.py
@@ -14,11 +14,11 @@
 DIRECT = 4
 TURN = 2
 EARLY = 3
-MIDDLE = 1
-MIX = (1, 1, 1)
+MIDDLE = 0
+PRE = 2
+LOW = 512
+MIX = (2, 1, 0, 0, 0)
 FIRST_MIX = ()
-LAST_EARLY = 4
-LAST_MIX = (2, 2, 2)
 MESH = pl.DeviceIdType.MESH
 F32 = jnp.float32
 BF16 = jnp.bfloat16
@@ -43,7 +43,7 @@
 
 
 def _kernel(norm, kern_hbm, cost_hbm, src_hbm, tgt_hbm, u_out, v_out, c_out,
-            kern, kern_t, cost, src, tgt, u_all, s_acc, lo_in, hi_in, x_out, x_in, t_out, t_in, vb_out, vb_in, w_acc, c_all, z_all,
+            kern, kern_t, cost, src, tgt, u_all, s_acc, lo_in, hi_in, x_out, x_in, t_out, t_in, vb_out, vb_in, vf_out, vf_in, w_acc, c_all, z_all,
             load_sem, tgt_sem, src_sem, lo_send, lo_recv, hi_send, hi_recv, x_send, x_recv,
             t_send, t_recv, v_send, v_recv, f_send, f_recv, c_send, c_recv, z_send, z_recv):
     row = lax.axis_index("row")
@@ -55,12 +55,11 @@
     level = {"col": (1 - chip) * 2 + core}
     above = {"row": 1 - row}
     rows, cols = kern.shape
-    mid = rows // 2
+    mid = LOW
     q = t_out.shape[1]
     me = row * 4 + col
     wide = cols // LOADS
     base = DIRECT * STEP
-    n_last = cols // STEP
 
     def load(hbm, buf, i):
         part = pl.ds(i * wide, wide)
@@ -98,13 +97,12 @@
                 for j, dev in enumerate((across, level, mate))]
 
     def hi_copy(g, p):
-        return remote(s_acc.at[g, :, pl.ds(mid, mid)], hi_in.at[g, p], hi_send.at[g], hi_recv.at[g, p], mate)
+        return remote(s_acc.at[g, :, pl.ds(mid, rows - mid)], hi_in.at[g, p], hi_send.at[g], hi_recv.at[g, p], mate)
 
     def chip_copy(g, p):
         return remote(x_out.at[g], x_in.at[g, p], x_send.at[g], x_recv.at[g, p], across)
 
     def spread(g, p):
-        hi_copy(g, p).start()
         for copy in lo_copies(g, p):
             copy.start()
         lo_in[g, p, col] = s_acc[g, :, 0:mid]
@@ -122,8 +120,9 @@
 
     def start_cols(g):
         u = u_all[g, :, 0:mid].astype(BF16)
-        for i in range(n_last):
-            t_out[g, :, line(i)] = _dot(u, kern[0:mid, line(i)])
+        for i in range(PRE):
+            part = send_cols(i)
+            t_out[g, :, part] = _dot(u, kern[0:mid, part])
 
     def finish_hi(g, p):
         chip_copy(g, p).wait_recv()
@@ -136,36 +135,34 @@
             copy.wait_send()
 
 
-    def add_cols(g, part):
-        t_out[g, :, part] += _dot(u_all[g, :, mid:rows].astype(BF16), kern[mid:rows, part])
+    def send_cols(i):
+        return turn_cols(1 - row, i) if i < TURN else line(i - TURN)
 
     def t_copy(g, p, i):
-        part = turn_cols(1 - row, i) if i < TURN else line(i - TURN)
+        part = send_cols(i)
         return remote(t_out.at[g, :, part], t_in.at[g, p, :, part], t_send.at[g, i], t_recv.at[g, p, i], above)
 
     def v_copy(g, k):
         part = turn_slot(row, k)
         return remote(vb_out.at[g, :, part], vb_in.at[g, :, part], v_send.at[g, k], v_recv.at[g, k], above)
 
-    def f_copy(g, p, i):
-        return remote(t_out.at[g, :, line(i)], t_in.at[g, p, :, line(i)], f_send.at[g, i], f_recv.at[g, i], above)
+    def f_copy(g, k):
+        return remote(vf_out.at[g, :, turn_slot(row, k)], vf_in.at[g, :, turn_slot(row, k)], f_send.at[g, k], f_recv.at[g, k], above)
 
     def send_ops(g, p):
         def send(i):
-            add_cols(g, turn_cols(1 - row, i) if i < TURN else line(i - TURN))
+            part = send_cols(i)
+            if i < PRE:
+                t_out[g, :, part] += _dot(u_all[g, :, mid:rows].astype(BF16), kern[mid:rows, part])
+            else:
+                t_out[g, :, part] = _dot(u_all[g].astype(BF16), kern[:, part])
             t_copy(g, p, i).start()
 
         def keep(k):
-            add_cols(g, turn_cols(row, k))
+            part = turn_cols(row, k)
+            t_out[g, :, part] = _dot(u_all[g].astype(BF16), kern[:, part])
 
         return [functools.partial(send, i) for i in range(TURN + DIRECT)] + [functools.partial(keep, k) for k in range(TURN)]
-
-    def last_send_ops(g, p):
-        def send(i):
-            add_cols(g, line(i))
-            f_copy(g, p, i).start()
-
-        return [functools.partial(send, i) for i in range(n_last)]
 
     def gather(g, vb, part, first):
         got = _dot(vb, kern_t[part])
@@ -174,43 +171,57 @@
         else:
             s_acc[g] += got
 
-    def take_ops(g, p):
+    def weigh(g, vb, part, first):
+        got = _dot_t(vb, cost[:, part])
+        if first:
+            w_acc[g] = got
+        else:
+            w_acc[g] += got
+
+    def take_ops(g, p, last=False):
+        use = weigh if last else gather
+
+        def scale(part):
+            return tgt[g * q:(g + 1) * q, part] / (t_out[g, :, part] + t_in[g, p, :, part])
+
         def own(k):
             t_copy(g, p, k).wait_recv()
             part = turn_cols(row, k)
-            vb = (tgt[g * q:(g + 1) * q, part] / (t_out[g, :, part] + t_in[g, p, :, part])).astype(BF16)
+            v = scale(part)
+            vb = v.astype(BF16)
             vb_out[g, :, turn_slot(row, k)] = vb
             v_copy(g, k).start()
-            gather(g, vb, part, k == 0)
+            if last:
+                vf_out[g, :, turn_slot(row, k)] = v
+                if g == GROUPS - 1 and k == TURN - 1:
+                    for h in range(GROUPS):
+                        for j in range(TURN):
+                            f_copy(h, j).start()
+                v_out[g * q:(g + 1) * q, part] = v
+            use(g, vb, part, k == 0)
 
         def both(i):
             t_copy(g, p, TURN + i).wait_recv()
             part = line(i)
-            vb = (tgt[g * q:(g + 1) * q, part] / (t_out[g, :, part] + t_in[g, p, :, part])).astype(BF16)
-            gather(g, vb, part, False)
+            v = scale(part)
+            if last:
+                v_out[g * q:(g + 1) * q, part] = v
+            use(g, v.astype(BF16), part, False)
 
         def back(k):
             v_copy(g, k).wait_recv()
-            gather(g, vb_in[g, :, turn_slot(1 - row, k)], turn_cols(1 - row, k), False)
-            if k == TURN - 1:
+            vb = vb_in[g, :, turn_slot(1 - row, k)]
+            part = turn_cols(1 - row, k)
+            if last or k < TURN - 1:
+                use(g, vb, part, False)
+            else:
+                s_acc[g, :, mid:rows] += _dot(vb, kern_t[part, mid:rows])
+                hi_copy(g, 1 - p).start()
+                s_acc[g, :, 0:mid] += _dot(vb, kern_t[part, 0:mid])
                 spread(g, 1 - p)
 
         return ([functools.partial(own, k) for k in range(TURN)] + [functools.partial(both, i) for i in range(DIRECT)]
                 + [functools.partial(back, k) for k in range(TURN)])
-
-    def last_take_ops(g, p):
-        def take(i):
-            f_copy(g, p, i).wait_recv()
-            part = line(i)
-            v = tgt[g * q:(g + 1) * q, part] / (t_out[g, :, part] + t_in[g, p, :, part])
-            v_out[g * q:(g + 1) * q, part] = v
-            got = _dot_t(v.astype(BF16), cost[:, part])
-            if i == 0:
-                w_acc[g] = got
-            else:
-                w_acc[g] += got
-
-        return [functools.partial(take, i) for i in range(n_last)]
 
     def sent(g, p):
         for i in range(TURN + DIRECT):
@@ -298,7 +309,7 @@
     lax.fori_loop(1, SWEEPS - 1, sweep, 0)
 
     p = (SWEEPS - 1) % 2
-    merge(last_send_ops(0, p), take_ops(1, 1 - p)[seen:], MIX)
+    merge(send_ops(0, p), take_ops(1, 1 - p)[seen:], MIX)
     settle(0, p)
     u_out[0:q] = u_all[0]
     sent(1, 1 - p)
@@ -306,19 +317,18 @@
     for i in range(LOADS):
         load(cost_hbm, cost, i).wait()
     cost[...] = kern[...] * cost[...]
-    takes = last_take_ops(0, p)
-    run(takes[:LAST_EARLY])
+    takes = take_ops(0, p, True)
+    run(takes[:EARLY])
     finish_lo(1, p)
     start_cols(1)
+    run(takes[EARLY:seen])
     finish_hi(1, p)
-    merge(last_send_ops(1, p), takes[LAST_EARLY:], LAST_MIX)
+    merge(send_ops(1, p), takes[seen:], MIX)
     settle(1, p)
     u_out[q:2 * q] = u_all[1]
-    run(last_take_ops(1, p))
-    for g in range(GROUPS):
-        for i in range(n_last):
-            f_copy(g, p, i).wait_send()
-    c_all[me] = jnp.broadcast_to(cost_row(0) + cost_row(1), (8, 128))
+    row_0 = cost_row(0)
+    run(take_ops(1, p, True))
+    c_all[me] = jnp.broadcast_to(row_0 + cost_row(1), (8, 128))
 
     def share(d):
         peer = lax.rem(me + d, 8)
@@ -327,6 +337,11 @@
 
     for d in range(1, 8):
         share(d).start()
+    for g in range(GROUPS):
+        for k in range(TURN):
+            f_copy(g, k).wait()
+            v_out[g * q:(g + 1) * q, turn_cols(1 - row, k)] = vf_in[g, :, turn_slot(1 - row, k)]
+        sent(g, p)
     for d in range(1, 8):
         share(d).wait()
     grand = c_all[0]
@@ -343,7 +358,8 @@
         rows, cols = kernel.shape
         batch = src_mass.shape[1]
         q = batch // GROUPS
-        mid = rows // 2
+        mid = LOW
+        top = rows - LOW
         norm = float(rows * row_size * cols * col_size)
         dma = pltpu.SemaphoreType.DMA
         hbm = pl.BlockSpec(memory_space=pltpu.HBM)
@@ -358,20 +374,22 @@
             pltpu.VMEM((GROUPS, q, rows), F32),
             pltpu.VMEM((GROUPS, q, rows), F32),
             pltpu.VMEM((GROUPS, 2, 4, q, mid), F32),
-            pltpu.VMEM((GROUPS, 2, q, mid), F32),
-            pltpu.VMEM((GROUPS, q, mid), F32),
-            pltpu.VMEM((GROUPS, 2, q, mid), F32),
+            pltpu.VMEM((GROUPS, 2, q, top), F32),
+            pltpu.VMEM((GROUPS, q, top), F32),
+            pltpu.VMEM((GROUPS, 2, q, top), F32),
             pltpu.VMEM((GROUPS, q, cols), F32),
             pltpu.VMEM((GROUPS, 2, q, cols), F32),
             pltpu.VMEM((GROUPS, q, turn), BF16),
             pltpu.VMEM((GROUPS, q, turn), BF16),
+            pltpu.VMEM((GROUPS, q, turn), F32),
+            pltpu.VMEM((GROUPS, q, turn), F32),
             pltpu.VMEM((GROUPS, q, rows), F32),
             pltpu.VMEM((8, 8, 128), F32),
             pltpu.VMEM((4, 8, 128), F32),
             dma((LOADS,)), dma, dma,
             dma((GROUPS, 3)), dma((GROUPS, 2, 3)), dma((GROUPS,)), dma((GROUPS, 2)), dma((GROUPS,)), dma((GROUPS, 2)),
             dma((GROUPS, TURN + DIRECT)), dma((GROUPS, 2, TURN + DIRECT)), dma((GROUPS, TURN)), dma((GROUPS, TURN)),
-            dma((GROUPS, cols // STEP)), dma((GROUPS, cols // STEP)), dma((7,)), dma((7,)), dma((3,)), dma((3,)),
+            dma((GROUPS, TURN)), dma((GROUPS, TURN)), dma((7,)), dma((7,)), dma((3,)), dma((3,)),
         ]
         u_shape = jax.ShapeDtypeStruct((batch, rows), F32)
         v_shape = jax.ShapeDtypeStruct((batch, cols), F32)

time: 88.6 us -> 87.2 us (0.984)
  Pallas kernels: 87.7 us -> 86.3 us
    pallas_call x1, Pallas kernels: 86.9 us -> 85.4 us  [local_fn(): pl.pallas_call(functools.partial(_kernel, norm), out_shape=(u_shape, v_sh...]
where the time goes in v5:
time: 87.2 us; the launch traced here: 87.1 us
  Pallas kernels  86.3 us (99%)
    pallas_call x1, Pallas kernels, local_fn(): pl.pallas_call(functools.partial(_kernel, norm), out_shape=(u_shape, v_sh...  85.4 us

profile of v5, /device:TPU:0, one launch (start us, length us, event | category | flops | bytes accessed | tf_op | source)
XLA Modules:
  0.0 87.1 jit_solution(7736385817050896571)
XLA Ops:
  0.6 85.4 %sinkhorn.1 = (f32[32,1024]{1,0:T(8,128)S(1)}, f32[32,4096]{1,0:T(8,128)S(1)}, f32[8,128]{1,0:T(8,128)S(1)}) custom-call(bf16[1024,4096]{1,0:T(8,128)(2,1)} %kern_hbm.1, bf16[1024,4096]{1,0:T(8,128)(2,1)} %cost_hbm.1, f32[32,1024]{1,0:T(8,128)} %bitcast.5, f32[32,4096]{1,0:T(8,128)} %bitcast.4), custom_call_target="tpu_custom_call" | custom-call | tf_op jit(solution)/shard_map/sinkhorn/pallas_call | solution.py:396
  86.1 0.9 emit.1

commit v6 on v5

--- a/solution.py
+++ b/solution.py
@@ -18,6 +18,7 @@
 PRE = 2
 LOW = 512
 MIX = (2, 1, 0, 0, 0)
+KEEP = 5
 FIRST_MIX = ()
 MESH = pl.DeviceIdType.MESH
 F32 = jnp.float32
@@ -282,10 +283,11 @@
     run(send_ops(0, 0))
     start_cols(1)
     run(take_ops(0, 0)[:TURN])
-    merge(send_ops(1, 0), take_ops(0, 0)[TURN:], FIRST_MIX)
+    merge(send_ops(1, 0)[:KEEP], take_ops(0, 0)[TURN:], FIRST_MIX)
     relay(0, 1)
+    run(send_ops(1, 0)[KEEP:])
+    run(take_ops(1, 0)[:EARLY])
     sent(0, 0)
-    run(take_ops(1, 0)[:EARLY])
     finish_lo(0, 1)
     start_cols(0)
     run(take_ops(1, 0)[EARLY:seen])
@@ -295,11 +297,12 @@
         p = lax.rem(step, 2)
         for g, pg, ph in ((0, p, 1 - p), (1, p, p)):
             h = 1 - g
-            merge(send_ops(g, pg), take_ops(h, ph)[seen:], MIX)
+            merge(send_ops(g, pg)[:KEEP], take_ops(h, ph)[seen:], MIX)
+            relay(h, 1 - ph)
+            run(send_ops(g, pg)[KEEP:])
             settle(g, pg)
+            run(take_ops(g, pg)[:EARLY])
             sent(h, ph)
-            relay(h, 1 - ph)
-            run(take_ops(g, pg)[:EARLY])
             finish_lo(h, 1 - ph)
             start_cols(h)
             run(take_ops(g, pg)[EARLY:seen])
@@ -309,11 +312,12 @@
     lax.fori_loop(1, SWEEPS - 1, sweep, 0)
 
     p = (SWEEPS - 1) % 2
-    merge(send_ops(0, p), take_ops(1, 1 - p)[seen:], MIX)
+    merge(send_ops(0, p)[:KEEP], take_ops(1, 1 - p)[seen:], MIX)
+    relay(1, p)
+    run(send_ops(0, p)[KEEP:])
     settle(0, p)
     u_out[0:q] = u_all[0]
     sent(1, 1 - p)
-    relay(1, p)
     for i in range(LOADS):
         load(cost_hbm, cost, i).wait()
     cost[...] = kern[...] * cost[...]

time: 87.2 us -> 86.6 us (level)
  no operation moved by 1% of the time
where the time goes in v6:
time: 86.6 us
  Pallas kernels  85.8 us (99%)
    pallas_call x1, Pallas kernels, local_fn(): pl.pallas_call(functools.partial(_kernel, norm), out_shape=(u_shape, v_sh...  84.9 us

profile of v6, /device:TPU:0, one launch (start us, length us, event | category | flops | bytes accessed | tf_op | source)
XLA Modules:
  0.0 86.6 jit_solution(15356226684724706013)
XLA Ops:
  0.6 84.9 %sinkhorn.1 = (f32[32,1024]{1,0:T(8,128)S(1)}, f32[32,4096]{1,0:T(8,128)S(1)}, f32[8,128]{1,0:T(8,128)S(1)}) custom-call(bf16[1024,4096]{1,0:T(8,128)(2,1)} %kern_hbm.1, bf16[1024,4096]{1,0:T(8,128)(2,1)} %cost_hbm.1, f32[32,1024]{1,0:T(8,128)} %bitcast.5, f32[32,4096]{1,0:T(8,128)} %bitcast.4), custom_call_target="tpu_custom_call" | custom-call | tf_op jit(solution)/shard_map/sinkhorn/pallas_call | solution.py:400
  85.5 0.9 emit.1

commit v7 on v6

--- a/solution.py
+++ b/solution.py
@@ -95,7 +95,7 @@
 
     def lo_copies(g, p):
         return [remote(s_acc.at[g, :, pl.ds(0, mid)], lo_in.at[g, p, col], lo_send.at[g, j], lo_recv.at[g, p, j], dev)
-                for j, dev in enumerate((across, level, mate))]
+                for j, dev in enumerate((level, across, mate))]
 
     def hi_copy(g, p):
         return remote(s_acc.at[g, :, pl.ds(mid, rows - mid)], hi_in.at[g, p], hi_send.at[g], hi_recv.at[g, p], mate)
@@ -322,12 +322,11 @@
         load(cost_hbm, cost, i).wait()
     cost[...] = kern[...] * cost[...]
     takes = take_ops(0, p, True)
-    run(takes[:EARLY])
+    run(takes[:TURN])
     finish_lo(1, p)
     start_cols(1)
-    run(takes[EARLY:seen])
     finish_hi(1, p)
-    merge(send_ops(1, p), takes[seen:], MIX)
+    merge(send_ops(1, p), takes[TURN:], MIX)
     settle(1, p)
     u_out[q:2 * q] = u_all[1]
     row_0 = cost_row(0)

time: 86.6 us -> 86.4 us (level)
  no operation moved by 1% of the time
where the time goes in v7:
time: 86.4 us; the launch traced here: 86.3 us
  Pallas kernels  85.5 us (99%)
    pallas_call x1, Pallas kernels, local_fn(): pl.pallas_call(functools.partial(_kernel, norm), out_shape=(u_shape, v_sh...  84.6 us

profile of v7, /device:TPU:0, one launch (start us, length us, event | category | flops | bytes accessed | tf_op | source)
XLA Modules:
  0.0 86.3 jit_solution(10834476068429345205)
XLA Ops:
  0.6 84.6 %sinkhorn.1 = (f32[32,1024]{1,0:T(8,128)S(1)}, f32[32,4096]{1,0:T(8,128)S(1)}, f32[8,128]{1,0:T(8,128)S(1)}) custom-call(bf16[1024,4096]{1,0:T(8,128)(2,1)} %kern_hbm.1, bf16[1024,4096]{1,0:T(8,128)(2,1)} %cost_hbm.1, f32[32,1024]{1,0:T(8,128)} %bitcast.5, f32[32,4096]{1,0:T(8,128)} %bitcast.4), custom_call_target="tpu_custom_call" | custom-call | tf_op jit(solution)/shard_map/sinkhorn/pallas_call | solution.py:399
  85.2 0.9 emit.1
